TPU v7x, 128 devices: a whole 4x4x4 slice. The times are simulated.
128 devices in a mesh: section: 32 (over y, z, core), tensor: 4 (over x).
Axes of the slice: x: 4, y: 4, z: 4, core: 2. Of those that a mesh axis runs over, the one named last changes fastest.
Arguments:
- section_input: bfloat16 [32, 512, 4096], P('section', 'tensor'), may hold values from -6 to 6
- history: bfloat16 [32, 7, 512, 4096], P('section', None, 'tensor'), may hold values from -6 to 6
- query_weight: bfloat16 [32, 4096, 3072], P('section', None, 'tensor'), may hold values from -0.4 to 0.4
- key_weight: bfloat16 [32, 4096, 512], P('section', None, 'tensor'), may hold values from -0.4 to 0.4
- value_weight: bfloat16 [32, 4096, 512], P('section', None, 'tensor'), may hold values from -0.09375 to 0.09375
- output_weight: bfloat16 [32, 3072, 4096], P('section', 'tensor'), may hold values from -0.5 to 0.5
- mix_weights: float32 [32, 8], replicated, may hold values from 0.2 to 0.6
Outputs:
- next_input: bfloat16 [32, 512, 4096], P('section', 'tensor')
All inputs are finite; a program needn't handle non-finite values.
Results may differ from a plain program's by a relative error of at most 0.013.
The roundings to bfloat16 on the way count: a program that leaves them out, or rounds other values in their place, can miss the bound.
Values may be sent and summed in bfloat16 or wider, within the bound.
No kernel may reach another device: no remote copies, remote signals or barrier semaphores. Data moves between devices by JAX's collectives and lax.ppermute only.
A program may use at most 128 MiB of HBM per device.

v0:
```python
import jax
import jax.numpy as jnp
from jax import lax
from jax.experimental import pallas as pl
from jax.experimental.pallas import tpu as pltpu
from jax.sharding import PartitionSpec as P


HEAD_DIM = 64
LANES = 128
LOG2_E = 1.4426950408889634
DILATION_STRIDE = 4
ROW = 2 * DILATION_STRIDE
COLUMN_PIECES = 2
PROJECTED_COLUMNS = 1024
MIB = 1 << 20
BF16, F32 = jnp.bfloat16, jnp.float32
BLOCK_OFFSETS = (0, 3, 1, 2)


def around(value, steps):
    count = lax.axis_size("tensor")
    return lax.ppermute(value, "tensor", [(i, (i + steps) % count) for i in range(count)])


def sent(value, sources, steps):
    return lax.ppermute(value, "section", [(i, i + steps(i)) for i in sources])


def to_next_section(block):
    count = lax.axis_size("section")
    return lax.ppermute(block, "section", [(i, (i + 1) % count) for i in range(count)])


def on_chip(body, outs, *args, limit=20, scratch=(), spaces=None):
    spaces = [pltpu.VMEM] * len(args) if spaces is None else spaces
    args = [
        value if space == pltpu.SMEM else pltpu.with_memory_space_constraint(value, space)
        for value, space in zip(args, spaces)
    ]
    return pl.pallas_call(
        body,
        out_shape=[pltpu.VMEM(shape, dtype) for shape, dtype in outs],
        in_specs=[pl.BlockSpec(memory_space=space) for space in spaces],
        out_specs=[pl.BlockSpec(memory_space=pltpu.VMEM)] * len(outs),
        scratch_shapes=list(scratch),
        compiler_params=pltpu.CompilerParams(vmem_limit_bytes=limit * MIB),
    )(*args)


def normalize_kernel(rows_ref, out):
    for start in range(0, out.shape[0], 16):
        rows = slice(start, start + 16)
        values = rows_ref[rows, :].astype(F32)
        inv_scale = lax.rsqrt(jnp.mean(values * values, axis=-1, keepdims=True) + 1e-05)
        out[rows, :] = (values * inv_scale).astype(BF16)


def load_kernel(wq, wk, wv, wo, inward, outward, sems):
    q, k = wq.shape[1], wk.shape[1]
    copies = [
        pltpu.make_async_copy(wq, inward.at[:, :q], sems.at[0]),
        pltpu.make_async_copy(wk, inward.at[:, q : q + k], sems.at[1]),
        pltpu.make_async_copy(wv, inward.at[:, q + k :], sems.at[2]),
        pltpu.make_async_copy(wo, outward, sems.at[3]),
    ]
    for copy in copies:
        copy.start()
    for copy in copies:
        copy.wait()


def place_in_grid():
    section = lax.axis_index("section")
    return section, section // ROW, section % ROW < DILATION_STRIDE


def coefficients(weights, section):
    at = lax.broadcasted_iota(jnp.int32, weights.shape, 1) == section
    column = jnp.sum(jnp.where(at, weights[...], F32(0.0)), axis=1, keepdims=True)
    return lambda k: column[k : k + 1, :]


def kept(condition, value):
    return jnp.where(condition, value, jnp.zeros_like(value))


def slots_kernel(pick):
    def kernel(history, *refs):
        outs, sems = refs[:-1], refs[-1]
        copies = [
            pltpu.make_async_copy(history.at[slot - 1], out, sems.at[i])
            for i, (slot, out) in enumerate(zip(pick(), outs))
        ]
        for copy in copies:
            copy.start()
        for copy in copies:
            copy.wait()

    return kernel


def first_slots():
    _, row, low = place_in_grid()
    return jnp.where(row < 2, jnp.where(low, 5, 3), jnp.where(low, 3, 1)), jnp.where(low, 7, 5)


def later_slots():
    _, _, low = place_in_grid()
    return jnp.where(low, 3, 1), 6, 4, 2, 1


def weighted(out, *terms):
    for start in range(0, out.shape[0], 16):
        rows = slice(start, start + 16)
        total = None
        for factor, block in terms:
            term = block[rows, :].astype(F32)
            term = term if factor is None else factor * term
            total = term if total is None else total + term
        out[rows, :] = total.astype(out.dtype)


def two_rows_kernel(weights, straight, crossed, out):
    section, _, low = place_in_grid()
    factor = coefficients(weights, jnp.minimum(section + 2 * ROW, weights.shape[1] - 1))
    weighted(out, (factor(4), straight), (jnp.where(low, factor(3), factor(5)), crossed))


def one_row_kernel(weights, straight, crossed_early, crossed_late, carried, out):
    section, row, low = place_in_grid()
    factor = coefficients(weights, jnp.minimum(section + ROW, weights.shape[1] - 1))
    crossed = jnp.where(low, factor(1), factor(3))
    weighted(
        out,
        (factor(2), straight),
        (kept(row == 2, crossed), crossed_early),
        (kept(row < 2, crossed), crossed_late),
        (None, carried),
    )


def cross_last_kernel(weights, far, same_row, out):
    section, row, low = place_in_grid()
    target = jnp.where(low, section + DILATION_STRIDE, jnp.maximum(section - DILATION_STRIDE, 0))
    factor = coefficients(weights, target)
    weighted(
        out,
        (kept(row == 3, jnp.where(low, factor(7), factor(5))), far),
        (kept(low, factor(1)), same_row),
    )


def projected(rows, inward):
    out = jnp.dot(rows, inward, preferred_element_type=F32)
    q_width = inward.shape[1] - 2 * LANES
    query = out[:, :q_width].astype(BF16)
    low = lax.broadcasted_iota(jnp.int32, (1, LANES), 1) < HEAD_DIM
    parts = []
    for start in (q_width, q_width + LANES):
        pair = out[:, start : start + LANES]
        swapped = pltpu.roll(pair, HEAD_DIM, 1)
        zero = jnp.zeros_like(pair)
        parts += [
            jnp.where(low, pair, zero),
            jnp.where(low, zero, swapped),
            jnp.where(low, swapped, zero),
            jnp.where(low, zero, pair),
        ]
    return query, jnp.concatenate([part.astype(BF16) for part in parts], axis=1)


def project_kernel(*refs):
    *blocks, inward, query_ref, kv_ref = refs
    rows = jnp.concatenate([block[...] for block in blocks], axis=0)
    query_ref[...], kv_ref[...] = projected(rows, inward[...])


def attended(query, kv, block):
    rows, place, ring = query.shape[0], lax.axis_index("tensor"), len(BLOCK_OFFSETS)
    row = lax.broadcasted_iota(jnp.int32, (rows, 1), 0) + (place + block) % ring * rows
    lane = lax.broadcasted_iota(jnp.int32, (1, rows), 1)
    key = jnp.concatenate([lane + (place + b) % ring * rows for b in BLOCK_OFFSETS], axis=1)
    bias = jnp.where(row >= key, F32(0.0), F32(-1e30))
    low = lax.broadcasted_iota(jnp.int32, (kv.shape[0], LANES), 1) < HEAD_DIM
    ones = [jnp.where(side, F32(1.0), F32(0.0)).astype(BF16) for side in (low, ~low)]
    out = []
    pairs = query.shape[1] // LANES
    for group in range(2):
        keys, values = [], []
        for side in range(2):
            at = (2 * group + side) * LANES
            keys.append(kv[:, at : at + LANES])
            values.append(jnp.concatenate([kv[:, 4 * LANES + at : 5 * LANES + at], ones[side]], axis=1))
        values = jnp.concatenate(values, axis=0)
        for pair in range(group * pairs // 2, (group + 1) * pairs // 2):
            q_pair = query[:, pair * LANES : (pair + 1) * LANES]
            weights = []
            for side in range(2):
                scores = lax.dot_general(q_pair, keys[side], (((1,), (1,)), ((), ())), preferred_element_type=F32)
                scores = scores + bias
                highest = jnp.max(scores, axis=-1, keepdims=True)
                weights.append(jnp.exp2((scores - highest) * F32(HEAD_DIM**-0.5 * LOG2_E)).astype(BF16))
            summed = jnp.dot(jnp.concatenate(weights, axis=1), values, preferred_element_type=F32)
            out.append((summed[:, :LANES] * (1.0 / summed[:, LANES:])).astype(BF16))
    return jnp.concatenate(out, axis=1)


def put_projected(heads, outward, top_ref, bottom_ref):
    half, width = top_ref.shape
    step = PROJECTED_COLUMNS
    for start in range(0, width, step):
        part = jnp.dot(heads, outward[:, start : start + step], preferred_element_type=F32).astype(BF16)
        top_ref[:, start : start + step] = part[:half]
        bottom_ref[:, start : start + step] = part[half:]


def opposite_kernel(top, bottom, inward, kv0, kv1, outward, out_top, out_bottom, kv_ref):
    rows = jnp.concatenate([top[...], bottom[...]], axis=0)
    query, kv3 = projected(rows, inward[...])
    kv_ref[...] = kv3
    kv = jnp.concatenate([kv0[...], kv1[...], kv3], axis=0)
    put_projected(attended(query, kv, BLOCK_OFFSETS[3]), outward, out_top, out_bottom)


def sides_kernel(query, kv0, kv1, kv3, outward, left_top, left_bottom, right_top, right_bottom):
    kv = jnp.concatenate([kv0[...], kv1[...], kv3[...]], axis=0)
    rows = query.shape[0] // 2
    put_projected(attended(query[:rows, :], kv, BLOCK_OFFSETS[1]), outward, left_top, left_bottom)
    put_projected(attended(query[rows:, :], kv, BLOCK_OFFSETS[2]), outward, right_top, right_bottom)


def own_kernel(query, kv0, kv1, kv3, outward, top, bottom):
    kv = jnp.concatenate([kv0[...], kv1[...], kv3[...]], axis=0)
    put_projected(attended(query[...], kv, BLOCK_OFFSETS[0]), outward, top, bottom)


def merge_kernel(right_top, right_bottom, left_top, left_bottom, from_left, from_right, *outs):
    half, width = right_top.shape
    count = len(outs) // 2
    step = width // count
    for c in range(count):
        cols = slice(c * step, (c + 1) * step)
        to_right, to_left = outs[c], outs[count + c]
        to_right[:half, :] = (right_top[:, cols].astype(F32) + from_left[:, cols].astype(F32)).astype(BF16)
        to_right[half:, :] = right_bottom[:, cols]
        to_left[:half, :] = left_top[:, cols]
        to_left[half:, :] = (left_bottom[:, cols].astype(F32) + from_right[:, cols].astype(F32)).astype(BF16)


def finish(piece):
    def kernel(weights, tokens, top, bottom, from_left, from_right, arrived, straight, crossed, out):
        half, step = top.shape[0], out.shape[1]
        section, row, _ = place_in_grid()
        factor = coefficients(weights, section)
        first, far = factor(0), kept(row == 3, factor(6))
        cols = slice(piece * step, (piece + 1) * step)
        for own, base in ((top, 0), (bottom, half)):
            for start in range(0, half, 16):
                rows, here = slice(base + start, base + start + 16), slice(start, start + 16)
                attention_sum = (
                    own[here, cols].astype(F32) + from_left[rows, :].astype(F32) + from_right[rows, :].astype(F32)
                )
                block_out = (tokens[rows, cols].astype(F32) + attention_sum).astype(BF16)
                past = arrived[rows, cols].astype(F32) + crossed[rows, cols].astype(F32)
                past = past + far * straight[rows, cols].astype(F32)
                out[rows, :] = (first * block_out.astype(F32) + past).astype(BF16)

    return kernel


def on_device(
    section_input, history, query_weight, key_weight, value_weight, output_weight, mix_weights
):
    token_rows = section_input[0]
    rows, width = token_rows.shape
    half, step = rows // 2, width // COLUMN_PIECES
    wq, wk, wv, wo = query_weight[0], key_weight[0], value_weight[0], output_weight[0]
    q_width, inward_width = wq.shape[1], wq.shape[1] + 2 * wk.shape[1]
    table = mix_weights.T
    half_block, block, kv_width = ((half, width), BF16), ((rows, width), BF16), 8 * LANES
    rows_of = lambda first, last: range(first * ROW, last * ROW)
    swap = lambda i: DILATION_STRIDE if i % ROW < DILATION_STRIDE else -DILATION_STRIDE

    (normed,) = on_chip(normalize_kernel, [block], token_rows, limit=6)
    left, right = around(normed, 1), around(normed, -1)
    opposite_top, opposite_bottom = around(left[:half], 1), around(right[half:], -1)

    stored = []
    for pick, count in ((first_slots, 2), (later_slots, 5)):
        stored += on_chip(
            slots_kernel(pick), [block] * count, history[0],
            limit=6, scratch=[pltpu.SemaphoreType.DMA((count,))], spaces=[pltpu.HBM],
        )
    early, far, late, far_straight, two_straight, one_straight, same_row = stored
    crossed_early = sent(early, rows_of(0, 3), swap)
    far_odd = sent(far, rows_of(0, 1), lambda i: 3 * ROW)
    crossed_late = sent(late, rows_of(0, 2), swap)
    far_even = sent(far_straight, rows_of(0, 1), lambda i: 3 * ROW)

    def combine(kernel, *blocks):
        return on_chip(kernel, [block], table, *blocks, limit=6)[0]

    two_rows = combine(two_rows_kernel, two_straight, crossed_early)
    carried = sent(two_rows, rows_of(0, 2), lambda i: ROW)
    last = combine(cross_last_kernel, far_odd, same_row)
    crossed_last = sent(last, [i for i in rows_of(0, 4) if i >= 3 * ROW or swap(i) > 0], swap)
    one_row = combine(one_row_kernel, one_straight, crossed_early, crossed_late, carried)
    arrived = sent(one_row, rows_of(0, 3), lambda i: ROW)

    inward, outward = on_chip(
        load_kernel, [((width, inward_width), BF16), (wo.shape, BF16)],
        wq, wk, wv, wo,
        limit=1, scratch=[pltpu.SemaphoreType.DMA((4,))], spaces=[pltpu.HBM] * 4,
    )
    q0, kv0 = on_chip(
        project_kernel, [((rows, q_width), BF16), ((rows, kv_width), BF16)], normed, inward,
        limit=12,
    )
    q1, kv1 = on_chip(
        project_kernel, [((2 * rows, q_width), BF16), ((2 * rows, kv_width), BF16)],
        left, right, inward, limit=16,
    )
    out3_top, out3_bottom, kv3 = on_chip(
        opposite_kernel, [half_block, half_block, ((rows, kv_width), BF16)],
        opposite_top, opposite_bottom, inward, kv0, kv1, outward,
    )
    from_left_merge, from_right_merge = around(out3_top, 1), around(out3_bottom, -1)
    left_out_top, left_out_bottom, right_out_top, right_out_bottom = on_chip(
        sides_kernel, [half_block] * 4, q1, kv0, kv1, kv3, outward
    )
    own_top, own_bottom = on_chip(own_kernel, [half_block] * 2, q0, kv0, kv1, kv3, outward)
    merged = on_chip(
        merge_kernel, [((rows, step), BF16)] * (2 * COLUMN_PIECES),
        right_out_top, right_out_bottom, left_out_top, left_out_bottom, from_left_merge, from_right_merge, limit=8,
    )
    pieces = []
    for c in range(COLUMN_PIECES):
        from_left = around(merged[c], 1)
        from_right = around(merged[COLUMN_PIECES + c], -1)
        (mixed,) = on_chip(
            finish(c), [((rows, step), BF16)], table, token_rows, own_top, own_bottom,
            from_left, from_right, arrived, far_even, crossed_last,
            limit=8,
        )
        pieces.append(to_next_section(mixed))
    return jnp.concatenate(pieces, axis=1)[None]


def solution(mesh):
    placed = (
        P("section", "tensor", None),
        P("section", None, "tensor", None),
        P("section", None, "tensor"),
        P("section", None, "tensor"),
        P("section", None, "tensor"),
        P("section", "tensor", None),
        P(),
    )

    return jax.shard_map(
        on_device,
        mesh=mesh,
        in_specs=placed,
        out_specs=P("section", "tensor", None),
        check_vma=False,
    )
```

profile of v0, /device:TPU:0, one launch (start us, length us, event | category | flops | bytes accessed | tf_op | source)
XLA Modules:
  0.0 115.6 jit_solution(1300518087241210725)
XLA Ops:
  0.0 1.6 %shard_map.82 = (bf16[128,4096]{1,0:T(8,128)(2,1)S(1)}, bf16[128,4096]{1,0:T(8,128)(2,1)S(1)}) custom-call(bf16[7,128,4096]{2,1,0:T(8,128)(2,1)} %bitcast.17), custom_call_target="tpu_custom_call" | custom-call | tf_op jit(solution)/shard_map/pallas_call | solution.py:41
  1.7 0.0 copy-start.1
  1.7 5.9 %collective-permute-start.8 = (bf16[128,4096]{1,0:T(8,128)(2,1)S(1)}, bf16[128,4096]{1,0:T(8,128)(2,1)S(1)}, u32[]{:S(2)}, u32[]{:S(2)}) collective-permute-start(bf16[128,4096]{1,0:T(8,128)(2,1)S(1)} %get-tuple-element.49), channel_id=1, source_target_pairs={{0,16},{4,20},{8,24},{12,28},{16,0},{20,4},{24,8},{28,12},{32,48},... | collective-permute-start | bytes 3145736 | tf_op jit(solution)/shard_map/ppermute | solution.py:27
  7.6 0.4 shard_map.73.refs_0_
  8.0 1.6 %collective-permute-start = (bf16[128,4096]{1,0:T(8,128)(2,1)S(1)}, bf16[128,4096]{1,0:T(8,128)(2,1)S(1)}, u32[]{:S(2)}, u32[]{:S(2)}) collective-permute-start(bf16[128,4096]{1,0:T(8,128)(2,1)S(1)} %shard_map.73.refs_0_), channel_id=1, source_target_pairs={{0,1},{1,2},{2,3},{3,0},{4,5},{5,6},{6,7},{7,4},{8,9},{9,10},{10,1... | collective-permute-start | bytes 3145736 | tf_op jit(solution)/shard_map/ppermute | solution.py:23
  9.5 1.7 %collective-permute-start.1 = (bf16[128,4096]{1,0:T(8,128)(2,1)S(1)}, bf16[128,4096]{1,0:T(8,128)(2,1)S(1)}, u32[]{:S(2)}, u32[]{:S(2)}) collective-permute-start(bf16[128,4096]{1,0:T(8,128)(2,1)S(1)} %shard_map.73.refs_0_), channel_id=1, source_target_pairs={{0,3},{1,0},{2,1},{3,2},{4,7},{5,4},{6,5},{7,6},{8,11},{9,8},{10,9... | collective-permute-start | bytes 3145736 | tf_op jit(solution)/shard_map/ppermute | solution.py:23
  11.3 1.3 %collective-permute-start.13 = (bf16[128,4096]{1,0:T(8,128)(2,1)S(1)}, bf16[128,4096]{1,0:T(8,128)(2,1)S(1)}, u32[]{:S(2)}, u32[]{:S(2)}) collective-permute-start(bf16[128,4096]{1,0:T(8,128)(2,1)S(1)} %get-tuple-element.53), channel_id=1, source_target_pairs={{0,96},{4,100},{8,104},{12,108},{16,112},{20,116},{24,120},{28,124... | collective-permute-start | bytes 3145736 | tf_op jit(solution)/shard_map/ppermute | solution.py:27
  12.6 2.5 %shard_map.81 = (bf16[128,4096]{1,0:T(8,128)(2,1)S(1)}, bf16[128,4096]{1,0:T(8,128)(2,1)S(1)}, bf16[128,4096]{1,0:T(8,128)(2,1)S(1)}, bf16[128,4096]{1,0:T(8,128)(2,1)S(1)}, bf16[128,4096]{1,0:T(8,128)(2,1)S(1)}) custom-call(bf16[7,128,4096]{2,1,0:T(8,128)(2,1)} %bitcast.18), custom_call_target="tpu_custom_call" | custom-call | tf_op jit(solution)/shard_map/pallas_call | solution.py:41
  15.2 4.4 %collective-permute-start.9 = (bf16[128,4096]{1,0:T(8,128)(2,1)S(1)}, bf16[128,4096]{1,0:T(8,128)(2,1)S(1)}, u32[]{:S(2)}, u32[]{:S(2)}) collective-permute-start(bf16[128,4096]{1,0:T(8,128)(2,1)S(1)} %get-tuple-element.50), channel_id=1, source_target_pairs={{0,16},{4,20},{8,24},{12,28},{16,0},{20,4},{24,8},{28,12},{32,48},... | collective-permute-start | bytes 3145736 | tf_op jit(solution)/shard_map/ppermute | solution.py:27
  19.5 12.0 %collective-permute-done.8.crossed.crossed_early = bf16[128,4096]{1,0:T(8,128)(2,1)S(1)} collective-permute-done((bf16[128,4096]{1,0:T(8,128)(2,1)S(1)}, bf16[128,4096]{1,0:T(8,128)(2,1)S(1)}, u32[]{:S(2)}, u32[]{:S(2)}) %collective-permute-start.8) | collective-permute-done | bytes 1048608 | tf_op jit(solution)/shard_map/ppermute | solution.py:27
  31.6 0.6 shard_map.83
  32.1 3.5 %collective-permute-start.10 = (bf16[128,4096]{1,0:T(8,128)(2,1)S(1)}, bf16[128,4096]{1,0:T(8,128)(2,1)S(1)}, u32[]{:S(2)}, u32[]{:S(2)}) collective-permute-start(bf16[128,4096]{1,0:T(8,128)(2,1)S(1)} %shard_map.83), channel_id=1, source_target_pairs={{0,32},{4,36},{8,40},{12,44},{16,48},{20,52},{24,56},{28,60},{32,6... | collective-permute-start | bytes 3145736 | tf_op jit(solution)/shard_map/ppermute | solution.py:27
  35.7 0.0 collective-permute-done.refs_0_
  35.8 1.6 %collective-permute-start.2 = (bf16[64,4096]{1,0:T(8,128)(2,1)S(1)}, bf16[64,4096]{1,0:T(8,128)(2,1)S(1)}, u32[]{:S(2)}, u32[]{:S(2)}) collective-permute-start(bf16[64,4096]{1,0:T(8,128)(2,1)S(1)} %slice.8), channel_id=1, source_target_pairs={{0,1},{1,2},{2,3},{3,0},{4,5},{5,6},{6,7},{7,4},{8,9},{9,10},{10,1... | collective-permute-start | bytes 1572872 | tf_op jit(solution)/shard_map/ppermute | solution.py:23
  37.3 0.0 collective-permute-done.1.refs_1_
  37.4 1.8 %collective-permute-start.3 = (bf16[64,4096]{1,0:T(8,128)(2,1)S(1)}, bf16[64,4096]{1,0:T(8,128)(2,1)S(1)}, u32[]{:S(2)}, u32[]{:S(2)}) collective-permute-start(bf16[64,4096]{1,0:T(8,128)(2,1)S(1)} %slice.9), channel_id=1, source_target_pairs={{0,3},{1,0},{2,1},{3,2},{4,7},{5,4},{6,5},{7,6},{8,11},{9,8},{10,9... | collective-permute-start | bytes 1572872 | tf_op jit(solution)/shard_map/ppermute | solution.py:23
  39.2 1.3 %collective-permute-start.12 = (bf16[128,4096]{1,0:T(8,128)(2,1)S(1)}, bf16[128,4096]{1,0:T(8,128)(2,1)S(1)}, u32[]{:S(2)}, u32[]{:S(2)}) collective-permute-start(bf16[128,4096]{1,0:T(8,128)(2,1)S(1)} %get-tuple-element.52), channel_id=1, source_target_pairs={{0,96},{4,100},{8,104},{12,108},{16,112},{20,116},{24,120},{28,124... | collective-permute-start | bytes 3145736 | tf_op jit(solution)/shard_map/ppermute | solution.py:27
  40.5 0.6 shard_map.85
  41.1 7.9 %collective-permute-done.2.top = bf16[64,4096]{1,0:T(8,128)(2,1)S(1)} collective-permute-done((bf16[64,4096]{1,0:T(8,128)(2,1)S(1)}, bf16[64,4096]{1,0:T(8,128)(2,1)S(1)}, u32[]{:S(2)}, u32[]{:S(2)}) %collective-permute-start.2) | collective-permute-done | bytes 524320 | tf_op jit(solution)/shard_map/ppermute | solution.py:23
  49.0 4.9 %collective-permute-start.14 = (bf16[128,4096]{1,0:T(8,128)(2,1)S(1)}, bf16[128,4096]{1,0:T(8,128)(2,1)S(1)}, u32[]{:S(2)}, u32[]{:S(2)}) collective-permute-start(bf16[128,4096]{1,0:T(8,128)(2,1)S(1)} %shard_map.85), channel_id=1, source_target_pairs={{0,16},{4,20},{8,24},{12,28},{32,48},{36,52},{40,56},{44,60},{64,8... | collective-permute-start | bytes 3145736 | tf_op jit(solution)/shard_map/ppermute | solution.py:27
  53.9 5.3 %shard_map.74 = (bf16[4096,1024]{1,0:T(8,128)(2,1)S(1)}, bf16[768,4096]{1,0:T(8,128)(2,1)S(1)}) custom-call(bf16[4096,768]{1,0:T(8,128)(2,1)} %bitcast.19, bf16[4096,128]{1,0:T(8,128)(2,1)} %bitcast.21, bf16[4096,128]{1,0:T(8,128)(2,1)} %bitcast.22, bf16[768,4096]{1,0:T(8,128)(2,1)} %bitcast.20), custom_call_target="tpu_custom_call" | custom-call | tf_op jit(solution)/shard_map/pallas_call | solution.py:41
  59.2 1.3 %shard_map.75 = (bf16[128,768]{1,0:T(8,128)(2,1)S(1)}, bf16[128,1024]{1,0:T(8,128)(2,1)S(1)}) custom-call(bf16[128,4096]{1,0:T(8,128)(2,1)S(1)} %shard_map.73.refs_0_, bf16[4096,1024]{1,0:T(8,128)(2,1)S(1)} %get-tuple-element.31.refs_1_.refs_2_.inward), custom_call_target="tpu_custom_call" | custom-call | tf_op jit(solution)/shard_map/pallas_call | solution.py:41
  60.6 2.4 %shard_map.76 = (bf16[256,768]{1,0:T(8,128)(2,1)S(1)}, bf16[256,1024]{1,0:T(8,128)(2,1)S(1)}) custom-call(bf16[128,4096]{1,0:T(8,128)(2,1)S(1)} %collective-permute-done.refs_0_, bf16[128,4096]{1,0:T(8,128)(2,1)S(1)} %collective-permute-done.1.refs_1_, bf16[4096,1024]{1,0:T(8,128)(2,1)S(1)} %get-tuple-element.31.refs_1_.refs_2_.inward), custom_call_target="tpu_custom_call" | custom-call | tf_op jit(solution)/shard_map/pallas_call | solution.py:41
  63.0 3.4 %shard_map.77 = (bf16[64,4096]{1,0:T(8,128)(2,1)S(1)}, bf16[64,4096]{1,0:T(8,128)(2,1)S(1)}, bf16[128,1024]{1,0:T(8,128)(2,1)S(1)}) custom-call(bf16[64,4096]{1,0:T(8,128)(2,1)S(1)} %collective-permute-done.2.top, bf16[64,4096]{1,0:T(8,128)(2,1)S(1)} %collective-permute-done.3.bottom, bf16[4096,1024]{1,0:T(8,128)(2,1)S(1)} %get-tuple-element.31.refs_1_.refs_2_.inward, ...), custom_call_target="tpu_custom_call" | custom-call | tf_op jit(solution)/shard_map/pallas_call | solution.py:41
  66.4 0.4 collective-permute-start.4
  66.8 3.0 %collective-permute-start.5 = (bf16[64,4096]{1,0:T(8,128)(2,1)S(1)}, bf16[64,4096]{1,0:T(8,128)(2,1)S(1)}, u32[]{:S(2)}, u32[]{:S(2)}) collective-permute-start(bf16[64,4096]{1,0:T(8,128)(2,1)S(1)} %get-tuple-element.45), channel_id=1, source_target_pairs={{0,3},{1,0},{2,1},{3,2},{4,7},{5,4},{6,5},{7,6},{8,11},{9,8},{10,9... | collective-permute-start | bytes 1572872 | tf_op jit(solution)/shard_map/ppermute | solution.py:23
  69.7 0.0 collective-permute-done.10.carried
  69.8 1.1 shard_map.84
  70.8 3.5 %collective-permute-start.11 = (bf16[128,4096]{1,0:T(8,128)(2,1)S(1)}, bf16[128,4096]{1,0:T(8,128)(2,1)S(1)}, u32[]{:S(2)}, u32[]{:S(2)}) collective-permute-start(bf16[128,4096]{1,0:T(8,128)(2,1)S(1)} %shard_map.84), channel_id=1, source_target_pairs={{0,32},{4,36},{8,40},{12,44},{16,48},{20,52},{24,56},{28,60},{32,6... | collective-permute-start | bytes 3145736 | tf_op jit(solution)/shard_map/ppermute | solution.py:27
  74.3 4.2 %shard_map.79 = (bf16[64,4096]{1,0:T(8,128)(2,1)S(1)}, bf16[64,4096]{1,0:T(8,128)(2,1)S(1)}, bf16[64,4096]{1,0:T(8,128)(2,1)S(1)}, bf16[64,4096]{1,0:T(8,128)(2,1)S(1)}) custom-call(bf16[256,768]{1,0:T(8,128)(2,1)S(1)} %get-tuple-element.39.query, bf16[128,1024]{1,0:T(8,128)(2,1)S(1)} %get-tuple-element.33.kv0, bf16[256,1024]{1,0:T(8,128)(2,1)S(1)} %get-tuple-element.34.kv1, ...), custom_call_target="tpu_custom_call" | custom-call | tf_op jit(solution)/shard_map/pallas_call | solution.py:41
  78.5 0.0 collective-permute-done.4.from_left
  78.5 0.0 collective-permute-done.5.from_right
  78.6 0.3 shard_map.80
  78.8 0.1 collective-permute-start.16
  78.9 3.2 %collective-permute-start.17 = (bf16[128,2048]{1,0:T(8,128)(2,1)S(1)}, bf16[128,2048]{1,0:T(8,128)(2,1)S(1)}, u32[]{:S(2)}, u32[]{:S(2)}) collective-permute-start(bf16[128,2048]{1,0:T(8,128)(2,1)S(1)} %get-tuple-element.56), channel_id=1, source_target_pairs={{0,3},{1,0},{2,1},{3,2},{4,7},{5,4},{6,5},{7,6},{8,11},{9,8},{10,9... | collective-permute-start | bytes 1572872 | tf_op jit(solution)/shard_map/ppermute | solution.py:23
  82.1 3.2 %collective-permute-start.7 = (bf16[128,2048]{1,0:T(8,128)(2,1)S(1)}, bf16[128,2048]{1,0:T(8,128)(2,1)S(1)}, u32[]{:S(2)}, u32[]{:S(2)}) collective-permute-start(bf16[128,2048]{1,0:T(8,128)(2,1)S(1)} %get-tuple-element.47), channel_id=1, source_target_pairs={{0,3},{1,0},{2,1},{3,2},{4,7},{5,4},{6,5},{7,6},{8,11},{9,8},{10,9... | collective-permute-start | bytes 1572872 | tf_op jit(solution)/shard_map/ppermute | solution.py:23
  85.4 2.3 %shard_map.78 = (bf16[64,4096]{1,0:T(8,128)(2,1)S(1)}, bf16[64,4096]{1,0:T(8,128)(2,1)S(1)}) custom-call(bf16[128,768]{1,0:T(8,128)(2,1)S(1)} %get-tuple-element.32.query, bf16[128,1024]{1,0:T(8,128)(2,1)S(1)} %get-tuple-element.33.kv0, bf16[256,1024]{1,0:T(8,128)(2,1)S(1)} %get-tuple-element.34.kv1, bf16[128,1024]{1,0:T(8,128)(2,1)S(1)} %get-tuple-element.36.kv3, ...), custom_call_target="tpu_custom_call" | custom-call | tf_op jit(solution)/shard_map/pallas_call | solution.py:41
  87.6 7.3 %collective-permute-done.16.from_left = bf16[128,2048]{1,0:T(8,128)(2,1)S(1)} collective-permute-done((bf16[128,2048]{1,0:T(8,128)(2,1)S(1)}, bf16[128,2048]{1,0:T(8,128)(2,1)S(1)}, u32[]{:S(2)}, u32[]{:S(2)}) %collective-permute-start.16) | collective-permute-done | bytes 524320 | tf_op jit(solution)/shard_map/ppermute | solution.py:23
  94.9 0.0 collective-permute-done.17.from_right
  94.9 0.0 collective-permute-done.11.arrived
  94.9 0.6 shard_map.87
  95.5 0.1 collective-permute-start.18
  95.6 6.3 %collective-permute-done.6.from_left = bf16[128,2048]{1,0:T(8,128)(2,1)S(1)} collective-permute-done((bf16[128,2048]{1,0:T(8,128)(2,1)S(1)}, bf16[128,2048]{1,0:T(8,128)(2,1)S(1)}, u32[]{:S(2)}, u32[]{:S(2)}) %collective-permute-start.6) | collective-permute-done | bytes 524320 | tf_op jit(solution)/shard_map/ppermute | solution.py:23
  101.9 0.6 shard_map.86
  102.5 0.1 collective-permute-start.15
  102.6 4.9 %collective-permute-done.18 = bf16[128,2048]{1,0:T(8,128)(2,1)S(1)} collective-permute-done((bf16[128,2048]{1,0:T(8,128)(2,1)S(1)}, bf16[128,2048]{1,0:T(8,128)(2,1)S(1)}, u32[]{:S(2)}, u32[]{:S(2)}) %collective-permute-start.18) | collective-permute-done | bytes 524320 | tf_op jit(solution)/shard_map/ppermute | solution.py:32
  107.5 7.0 %collective-permute-done.15 = bf16[128,2048]{1,0:T(8,128)(2,1)S(1)} collective-permute-done((bf16[128,2048]{1,0:T(8,128)(2,1)S(1)}, bf16[128,2048]{1,0:T(8,128)(2,1)S(1)}, u32[]{:S(2)}, u32[]{:S(2)}) %collective-permute-start.15) | collective-permute-done | bytes 524320 | tf_op jit(solution)/shard_map/ppermute | solution.py:32
  114.5 1.1 maximum_bitcast_fusion
  (12 shorter events, 0.1 us)
Async XLA Ops:
  0.0 7.6 %copy-start = (bf16[1,128,4096]{2,1,0:T(8,128)(2,1)S(1)}, bf16[1,128,4096]{2,1,0:T(8,128)(2,1)}, u32[]{:S(2)}) copy-start(bf16[1,128,4096]{2,1,0:T(8,128)(2,1)} %param.7) | copy-start | bytes 3145732
  1.7 29.9 %copy-start.1 = (f32[32,8]{0,1:T(8,128)S(1)}, f32[32,8]{0,1:T(8,128)}, u32[]{:S(2)}) copy-start(f32[32,8]{0,1:T(8,128)} %param.13) | copy-start | bytes 3076
  1.7 29.9 %collective-permute-start.8 = (bf16[128,4096]{1,0:T(8,128)(2,1)S(1)}, bf16[128,4096]{1,0:T(8,128)(2,1)S(1)}, u32[]{:S(2)}, u32[]{:S(2)}) collective-permute-start(bf16[128,4096]{1,0:T(8,128)(2,1)S(1)} %get-tuple-element.49), channel_id=1, source_target_pairs={{0,16},{4,20},{8,24},{12,28},{16,0},{20,4},{24,8},{28,12},{32,48},... | collective-permute-start | bytes 3145736 | tf_op jit(solution)/shard_map/ppermute | solution.py:27
  8.0 27.7 %collective-permute-start = (bf16[128,4096]{1,0:T(8,128)(2,1)S(1)}, bf16[128,4096]{1,0:T(8,128)(2,1)S(1)}, u32[]{:S(2)}, u32[]{:S(2)}) collective-permute-start(bf16[128,4096]{1,0:T(8,128)(2,1)S(1)} %shard_map.73.refs_0_), channel_id=1, source_target_pairs={{0,1},{1,2},{2,3},{3,0},{4,5},{5,6},{6,7},{7,4},{8,9},{9,10},{10,1... | collective-permute-start | bytes 3145736 | tf_op jit(solution)/shard_map/ppermute | solution.py:23
  9.5 27.8 %collective-permute-start.1 = (bf16[128,4096]{1,0:T(8,128)(2,1)S(1)}, bf16[128,4096]{1,0:T(8,128)(2,1)S(1)}, u32[]{:S(2)}, u32[]{:S(2)}) collective-permute-start(bf16[128,4096]{1,0:T(8,128)(2,1)S(1)} %shard_map.73.refs_0_), channel_id=1, source_target_pairs={{0,3},{1,0},{2,1},{3,2},{4,7},{5,4},{6,5},{7,6},{8,11},{9,8},{10,9... | collective-permute-start | bytes 3145736 | tf_op jit(solution)/shard_map/ppermute | solution.py:23
  11.3 27.9 %collective-permute-start.13 = (bf16[128,4096]{1,0:T(8,128)(2,1)S(1)}, bf16[128,4096]{1,0:T(8,128)(2,1)S(1)}, u32[]{:S(2)}, u32[]{:S(2)}) collective-permute-start(bf16[128,4096]{1,0:T(8,128)(2,1)S(1)} %get-tuple-element.53), channel_id=1, source_target_pairs={{0,96},{4,100},{8,104},{12,108},{16,112},{20,116},{24,120},{28,124... | collective-permute-start | bytes 3145736 | tf_op jit(solution)/shard_map/ppermute | solution.py:27
  15.2 51.6 %collective-permute-start.9 = (bf16[128,4096]{1,0:T(8,128)(2,1)S(1)}, bf16[128,4096]{1,0:T(8,128)(2,1)S(1)}, u32[]{:S(2)}, u32[]{:S(2)}) collective-permute-start(bf16[128,4096]{1,0:T(8,128)(2,1)S(1)} %get-tuple-element.50), channel_id=1, source_target_pairs={{0,16},{4,20},{8,24},{12,28},{16,0},{20,4},{24,8},{28,12},{32,48},... | collective-permute-start | bytes 3145736 | tf_op jit(solution)/shard_map/ppermute | solution.py:27
  32.1 37.6 %collective-permute-start.10 = (bf16[128,4096]{1,0:T(8,128)(2,1)S(1)}, bf16[128,4096]{1,0:T(8,128)(2,1)S(1)}, u32[]{:S(2)}, u32[]{:S(2)}) collective-permute-start(bf16[128,4096]{1,0:T(8,128)(2,1)S(1)} %shard_map.83), channel_id=1, source_target_pairs={{0,32},{4,36},{8,40},{12,44},{16,48},{20,52},{24,56},{28,60},{32,6... | collective-permute-start | bytes 3145736 | tf_op jit(solution)/shard_map/ppermute | solution.py:27
  35.8 13.2 %collective-permute-start.2 = (bf16[64,4096]{1,0:T(8,128)(2,1)S(1)}, bf16[64,4096]{1,0:T(8,128)(2,1)S(1)}, u32[]{:S(2)}, u32[]{:S(2)}) collective-permute-start(bf16[64,4096]{1,0:T(8,128)(2,1)S(1)} %slice.8), channel_id=1, source_target_pairs={{0,1},{1,2},{2,3},{3,0},{4,5},{5,6},{6,7},{7,4},{8,9},{9,10},{10,1... | collective-permute-start | bytes 1572872 | tf_op jit(solution)/shard_map/ppermute | solution.py:23
  37.4 25.6 %collective-permute-start.3 = (bf16[64,4096]{1,0:T(8,128)(2,1)S(1)}, bf16[64,4096]{1,0:T(8,128)(2,1)S(1)}, u32[]{:S(2)}, u32[]{:S(2)}) collective-permute-start(bf16[64,4096]{1,0:T(8,128)(2,1)S(1)} %slice.9), channel_id=1, source_target_pairs={{0,3},{1,0},{2,1},{3,2},{4,7},{5,4},{6,5},{7,6},{8,11},{9,8},{10,9... | collective-permute-start | bytes 1572872 | tf_op jit(solution)/shard_map/ppermute | solution.py:23
  39.2 43.0 %collective-permute-start.12 = (bf16[128,4096]{1,0:T(8,128)(2,1)S(1)}, bf16[128,4096]{1,0:T(8,128)(2,1)S(1)}, u32[]{:S(2)}, u32[]{:S(2)}) collective-permute-start(bf16[128,4096]{1,0:T(8,128)(2,1)S(1)} %get-tuple-element.52), channel_id=1, source_target_pairs={{0,96},{4,100},{8,104},{12,108},{16,112},{20,116},{24,120},{28,124... | collective-permute-start | bytes 3145736 | tf_op jit(solution)/shard_map/ppermute | solution.py:27
  49.0 33.2 %collective-permute-start.14 = (bf16[128,4096]{1,0:T(8,128)(2,1)S(1)}, bf16[128,4096]{1,0:T(8,128)(2,1)S(1)}, u32[]{:S(2)}, u32[]{:S(2)}) collective-permute-start(bf16[128,4096]{1,0:T(8,128)(2,1)S(1)} %shard_map.85), channel_id=1, source_target_pairs={{0,16},{4,20},{8,24},{12,28},{32,48},{36,52},{40,56},{44,60},{64,8... | collective-permute-start | bytes 3145736 | tf_op jit(solution)/shard_map/ppermute | solution.py:27
  66.4 12.1 %collective-permute-start.4 = (bf16[64,4096]{1,0:T(8,128)(2,1)S(1)}, bf16[64,4096]{1,0:T(8,128)(2,1)S(1)}, u32[]{:S(2)}, u32[]{:S(2)}) collective-permute-start(bf16[64,4096]{1,0:T(8,128)(2,1)S(1)} %get-tuple-element.44), channel_id=1, source_target_pairs={{0,1},{1,2},{2,3},{3,0},{4,5},{5,6},{6,7},{7,4},{8,9},{9,10},{10,1... | collective-permute-start | bytes 1572872 | tf_op jit(solution)/shard_map/ppermute | solution.py:23
  66.8 11.8 %collective-permute-start.5 = (bf16[64,4096]{1,0:T(8,128)(2,1)S(1)}, bf16[64,4096]{1,0:T(8,128)(2,1)S(1)}, u32[]{:S(2)}, u32[]{:S(2)}) collective-permute-start(bf16[64,4096]{1,0:T(8,128)(2,1)S(1)} %get-tuple-element.45), channel_id=1, source_target_pairs={{0,3},{1,0},{2,1},{3,2},{4,7},{5,4},{6,5},{7,6},{8,11},{9,8},{10,9... | collective-permute-start | bytes 1572872 | tf_op jit(solution)/shard_map/ppermute | solution.py:23
  70.8 24.1 %collective-permute-start.11 = (bf16[128,4096]{1,0:T(8,128)(2,1)S(1)}, bf16[128,4096]{1,0:T(8,128)(2,1)S(1)}, u32[]{:S(2)}, u32[]{:S(2)}) collective-permute-start(bf16[128,4096]{1,0:T(8,128)(2,1)S(1)} %shard_map.84), channel_id=1, source_target_pairs={{0,32},{4,36},{8,40},{12,44},{16,48},{20,52},{24,56},{28,60},{32,6... | collective-permute-start | bytes 3145736 | tf_op jit(solution)/shard_map/ppermute | solution.py:27
  78.8 16.1 %collective-permute-start.16 = (bf16[128,2048]{1,0:T(8,128)(2,1)S(1)}, bf16[128,2048]{1,0:T(8,128)(2,1)S(1)}, u32[]{:S(2)}, u32[]{:S(2)}) collective-permute-start(bf16[128,2048]{1,0:T(8,128)(2,1)S(1)} %get-tuple-element.55), channel_id=1, source_target_pairs={{0,1},{1,2},{2,3},{3,0},{4,5},{5,6},{6,7},{7,4},{8,9},{9,10},{10,1... | collective-permute-start | bytes 1572872 | tf_op jit(solution)/shard_map/ppermute | solution.py:23
  78.9 16.0 %collective-permute-start.17 = (bf16[128,2048]{1,0:T(8,128)(2,1)S(1)}, bf16[128,2048]{1,0:T(8,128)(2,1)S(1)}, u32[]{:S(2)}, u32[]{:S(2)}) collective-permute-start(bf16[128,2048]{1,0:T(8,128)(2,1)S(1)} %get-tuple-element.56), channel_id=1, source_target_pairs={{0,3},{1,0},{2,1},{3,2},{4,7},{5,4},{6,5},{7,6},{8,11},{9,8},{10,9... | collective-permute-start | bytes 1572872 | tf_op jit(solution)/shard_map/ppermute | solution.py:23
  82.1 19.8 %collective-permute-start.6 = (bf16[128,2048]{1,0:T(8,128)(2,1)S(1)}, bf16[128,2048]{1,0:T(8,128)(2,1)S(1)}, u32[]{:S(2)}, u32[]{:S(2)}) collective-permute-start(bf16[128,2048]{1,0:T(8,128)(2,1)S(1)} %get-tuple-element.46), channel_id=1, source_target_pairs={{0,1},{1,2},{2,3},{3,0},{4,5},{5,6},{6,7},{7,4},{8,9},{9,10},{10,1... | collective-permute-start | bytes 1572872 | tf_op jit(solution)/shard_map/ppermute | solution.py:23
  82.1 19.7 %collective-permute-start.7 = (bf16[128,2048]{1,0:T(8,128)(2,1)S(1)}, bf16[128,2048]{1,0:T(8,128)(2,1)S(1)}, u32[]{:S(2)}, u32[]{:S(2)}) collective-permute-start(bf16[128,2048]{1,0:T(8,128)(2,1)S(1)} %get-tuple-element.47), channel_id=1, source_target_pairs={{0,3},{1,0},{2,1},{3,2},{4,7},{5,4},{6,5},{7,6},{8,11},{9,8},{10,9... | collective-permute-start | bytes 1572872 | tf_op jit(solution)/shard_map/ppermute | solution.py:23
  95.5 12.0 %collective-permute-start.18 = (bf16[128,2048]{1,0:T(8,128)(2,1)S(1)}, bf16[128,2048]{1,0:T(8,128)(2,1)S(1)}, u32[]{:S(2)}, u32[]{:S(2)}) collective-permute-start(bf16[128,2048]{1,0:T(8,128)(2,1)S(1)} %shard_map.87), channel_id=1, source_target_pairs={{0,4},{4,8},{8,12},{12,16},{16,20},{20,24},{24,28},{28,32},{32,36}... | collective-permute-start | bytes 1572872 | tf_op jit(solution)/shard_map/ppermute | solution.py:32
  102.5 12.0 %collective-permute-start.15 = (bf16[128,2048]{1,0:T(8,128)(2,1)S(1)}, bf16[128,2048]{1,0:T(8,128)(2,1)S(1)}, u32[]{:S(2)}, u32[]{:S(2)}) collective-permute-start(bf16[128,2048]{1,0:T(8,128)(2,1)S(1)} %shard_map.86), channel_id=1, source_target_pairs={{0,4},{4,8},{8,12},{12,16},{16,20},{20,24},{24,28},{28,32},{32,36}... | collective-permute-start | bytes 1572872 | tf_op jit(solution)/shard_map/ppermute | solution.py:32
where the time goes:
time: 116 us
  waiting for transfers between devices  45.4 us (39%)
  starting transfers between devices  41.6 us (36%)
  Pallas kernels  27.2 us (23%)
    pallas_call x15, Pallas kernels, on_chip(): pl.pallas_call(body, out_shape=[pltpu.VMEM(shape, dtype) for shape, dtype...  27.2 us
    ppermute x7, starting transfers between devices, sent(): return lax.ppermute(value, 'section', [(i, i + steps(i)) for i in sources])  24.9 us
    ppermute x10, waiting for transfers between devices, around(): lax.ppermute(value, 'tensor', [(i, (i + steps) % count) for i in range(co...  21.4 us
    ppermute x10, starting transfers between devices, around(): lax.ppermute(value, 'tensor', [(i, (i + steps) % count) for i in range(co...  16.5 us
    ppermute x7, waiting for transfers between devices, sent(): return lax.ppermute(value, 'section', [(i, i + steps(i)) for i in sources])  12 us
    ppermute x2, waiting for transfers between devices, to_next_section(): lax.ppermute(block, 'section', [(i, (i + 1) % count) for i in range(count)])  11.9 us
  transfers between devices with their start and end apart: 19, of which 6 were waited for; matrix products, arithmetic and copies ran while one was open for 0% of the time, Pallas kernels for 22%

commit v1 on v0

v1 whole, which is shorter than its diff:
```python
import jax
import jax.numpy as jnp
from jax import lax
from jax.experimental import pallas as pl
from jax.experimental.pallas import tpu as pltpu
from jax.sharding import PartitionSpec as P


HEAD_DIM = 64
LANES = 128
LOG2_E = 1.4426950408889634
DILATION_STRIDE = 4
ROW = 2 * DILATION_STRIDE
SPLIT = 5 / 8
PROJECTED_COLUMNS = 1024
MIB = 1 << 20
BF16, F32 = jnp.bfloat16, jnp.float32
BLOCK_OFFSETS = (0, 3, 1, 2)


def around(value, steps):
    count = lax.axis_size("tensor")
    return lax.ppermute(value, "tensor", [(i, (i + steps) % count) for i in range(count)])


def sent(value, sources, steps):
    return lax.ppermute(value, "section", [(i, i + steps(i)) for i in sources])


def to_next_section(block):
    count = lax.axis_size("section")
    return lax.ppermute(block, "section", [(i, (i + 1) % count) for i in range(count)])


def on_chip(body, outs, *args, limit=20, scratch=(), spaces=None):
    spaces = [pltpu.VMEM] * len(args) if spaces is None else spaces
    args = [
        value if space == pltpu.SMEM else pltpu.with_memory_space_constraint(value, space)
        for value, space in zip(args, spaces)
    ]
    return pl.pallas_call(
        body,
        out_shape=[pltpu.VMEM(shape, dtype) for shape, dtype in outs],
        in_specs=[pl.BlockSpec(memory_space=space) for space in spaces],
        out_specs=[pl.BlockSpec(memory_space=pltpu.VMEM)] * len(outs),
        scratch_shapes=list(scratch),
        compiler_params=pltpu.CompilerParams(vmem_limit_bytes=limit * MIB),
    )(*args)


def prologue_kernel(tokens, history, out, early, far, rows_ref, sems):
    token_copy = pltpu.make_async_copy(tokens, rows_ref, sems.at[0])
    token_copy.start()
    copies = [
        pltpu.make_async_copy(history.at[slot - 1], block, sems.at[1 + i])
        for i, (slot, block) in enumerate(zip(first_slots(), (early, far)))
    ]
    for copy in copies:
        copy.start()
    token_copy.wait()
    for start in range(0, out.shape[0], 16):
        rows = slice(start, start + 16)
        values = rows_ref[rows, :].astype(F32)
        inv_scale = lax.rsqrt(jnp.mean(values * values, axis=-1, keepdims=True) + 1e-05)
        out[rows, :] = (values * inv_scale).astype(BF16)
    for copy in copies:
        copy.wait()


def load_kernel(wk, wv, joined, sems):
    copies = [
        pltpu.make_async_copy(wk, joined.at[:, :LANES], sems.at[0]),
        pltpu.make_async_copy(wv, joined.at[:, LANES:], sems.at[1]),
    ]
    for copy in copies:
        copy.start()
    for copy in copies:
        copy.wait()


def place_in_grid():
    section = lax.axis_index("section")
    return section, section // ROW, section % ROW < DILATION_STRIDE


def coefficients(weights, section):
    at = lax.broadcasted_iota(jnp.int32, weights.shape, 1) == section
    column = jnp.sum(jnp.where(at, weights[...], F32(0.0)), axis=1, keepdims=True)
    return lambda k: column[k : k + 1, :]


def kept(condition, value):
    return jnp.where(condition, value, jnp.zeros_like(value))


def slots_kernel(history, *refs):
    outs, sems = refs[:-1], refs[-1]
    _, _, low = place_in_grid()
    slots = (jnp.where(low, 3, 1), 6, 4, 2, 1)
    copies = [
        pltpu.make_async_copy(history.at[slot - 1], out, sems.at[i])
        for i, (slot, out) in enumerate(zip(slots, outs))
    ]
    for copy in copies:
        copy.start()
    for copy in copies:
        copy.wait()


def first_slots():
    _, row, low = place_in_grid()
    return jnp.where(row < 2, jnp.where(low, 5, 3), jnp.where(low, 3, 1)), jnp.where(low, 7, 5)


def weighted(out, first_column, *terms):
    width = out.shape[1]
    for start in range(0, out.shape[0], 16):
        rows = slice(start, start + 16)
        total = None
        for factor, block in terms:
            first = first_column if block.shape[1] > width else 0
            term = block[rows, first : first + width].astype(F32)
            term = term if factor is None else factor * term
            total = term if total is None else total + term
        out[rows, :] = total.astype(out.dtype)


def two_rows_kernel(weights, straight, crossed, *outs):
    section, _, low = place_in_grid()
    factor = coefficients(weights, jnp.minimum(section + 2 * ROW, weights.shape[1] - 1))
    first = 0
    for out in outs:
        weighted(out, first, (factor(4), straight), (jnp.where(low, factor(3), factor(5)), crossed))
        first += out.shape[1]


def one_row(first_column):
    def kernel(weights, straight, crossed_early, crossed_late, carried, out):
        section, row, low = place_in_grid()
        factor = coefficients(weights, jnp.minimum(section + ROW, weights.shape[1] - 1))
        crossed = jnp.where(low, factor(1), factor(3))
        weighted(
            out,
            first_column,
            (factor(2), straight),
            (kept(row == 2, crossed), crossed_early),
            (kept(row < 2, crossed), crossed_late),
            (None, carried),
        )

    return kernel


def projected(rows, wq, joined):
    query = jnp.dot(rows, wq, preferred_element_type=F32).astype(BF16)
    out = jnp.dot(rows, joined, preferred_element_type=F32)
    low = lax.broadcasted_iota(jnp.int32, (1, LANES), 1) < HEAD_DIM
    parts = []
    for start in (0, LANES):
        pair = out[:, start : start + LANES]
        swapped = pltpu.roll(pair, HEAD_DIM, 1)
        zero = jnp.zeros_like(pair)
        parts += [
            jnp.where(low, pair, zero),
            jnp.where(low, zero, swapped),
            jnp.where(low, swapped, zero),
            jnp.where(low, zero, pair),
        ]
    return query, jnp.concatenate([part.astype(BF16) for part in parts], axis=1)


def project_kernel(*refs):
    *blocks, wq, joined, query_ref, kv_ref = refs
    rows = jnp.concatenate([block[...] for block in blocks], axis=0)
    query_ref[...], kv_ref[...] = projected(rows, wq[...], joined[...])


def attended(query, kv, block):
    rows, place, ring = query.shape[0], lax.axis_index("tensor"), len(BLOCK_OFFSETS)
    row = lax.broadcasted_iota(jnp.int32, (rows, 1), 0) + (place + block) % ring * rows
    lane = lax.broadcasted_iota(jnp.int32, (1, rows), 1)
    key = jnp.concatenate([lane + (place + b) % ring * rows for b in BLOCK_OFFSETS], axis=1)
    bias = jnp.where(row >= key, F32(0.0), F32(-1e30))
    low = lax.broadcasted_iota(jnp.int32, (kv.shape[0], LANES), 1) < HEAD_DIM
    ones = [jnp.where(side, F32(1.0), F32(0.0)).astype(BF16) for side in (low, ~low)]
    out = []
    pairs = query.shape[1] // LANES
    for group in range(2):
        keys, values = [], []
        for side in range(2):
            at = (2 * group + side) * LANES
            keys.append(kv[:, at : at + LANES])
            values.append(jnp.concatenate([kv[:, 4 * LANES + at : 5 * LANES + at], ones[side]], axis=1))
        values = jnp.concatenate(values, axis=0)
        for pair in range(group * pairs // 2, (group + 1) * pairs // 2):
            q_pair = query[:, pair * LANES : (pair + 1) * LANES]
            weights = []
            for side in range(2):
                scores = lax.dot_general(q_pair, keys[side], (((1,), (1,)), ((), ())), preferred_element_type=F32)
                scores = scores + bias
                highest = jnp.max(scores, axis=-1, keepdims=True)
                weights.append(jnp.exp2((scores - highest) * F32(HEAD_DIM**-0.5 * LOG2_E)).astype(BF16))
            summed = jnp.dot(jnp.concatenate(weights, axis=1), values, preferred_element_type=F32)
            out.append((summed[:, :LANES] * (1.0 / summed[:, LANES:])).astype(BF16))
    return jnp.concatenate(out, axis=1)


def put_projected(heads, outward, top_ref, bottom_ref):
    half, width = top_ref.shape
    step = PROJECTED_COLUMNS
    for start in range(0, width, step):
        part = jnp.dot(heads, outward[:, start : start + step], preferred_element_type=F32).astype(BF16)
        top_ref[:, start : start + step] = part[:half]
        bottom_ref[:, start : start + step] = part[half:]


def opposite_kernel(top, bottom, wq, joined, kv0, kv1, outward, out_top, out_bottom, kv_ref):
    rows = jnp.concatenate([top[...], bottom[...]], axis=0)
    query, kv3 = projected(rows, wq[...], joined[...])
    kv_ref[...] = kv3
    kv = jnp.concatenate([kv0[...], kv1[...], kv3], axis=0)
    put_projected(attended(query, kv, BLOCK_OFFSETS[3]), outward, out_top, out_bottom)


def sides_kernel(query, kv0, kv1, kv3, outward, left_top, left_bottom, right_top, right_bottom):
    kv = jnp.concatenate([kv0[...], kv1[...], kv3[...]], axis=0)
    rows = query.shape[0] // 2
    put_projected(attended(query[:rows, :], kv, BLOCK_OFFSETS[1]), outward, left_top, left_bottom)
    put_projected(attended(query[rows:, :], kv, BLOCK_OFFSETS[2]), outward, right_top, right_bottom)


def own_kernel(query, kv0, kv1, kv3, outward, top, bottom):
    kv = jnp.concatenate([kv0[...], kv1[...], kv3[...]], axis=0)
    put_projected(attended(query[...], kv, BLOCK_OFFSETS[0]), outward, top, bottom)


def merge_kernel(right_top, right_bottom, left_top, left_bottom, from_left, from_right, *outs):
    half = right_top.shape[0]
    count, start = len(outs) // 2, 0
    for c in range(count):
        cols = slice(start, start + outs[c].shape[1])
        start = cols.stop
        to_right, to_left = outs[c], outs[count + c]
        to_right[:half, :] = (right_top[:, cols].astype(F32) + from_left[:, cols].astype(F32)).astype(BF16)
        to_right[half:, :] = right_bottom[:, cols]
        to_left[:half, :] = left_top[:, cols]
        to_left[half:, :] = (left_bottom[:, cols].astype(F32) + from_right[:, cols].astype(F32)).astype(BF16)


def finish(first_column):
    def kernel(weights, tokens, top, bottom, from_left, from_right, arrived, straight, crossed, same_row, out):
        half = top.shape[0]
        section, row, low = place_in_grid()
        factor = coefficients(weights, section)
        cols = slice(first_column, first_column + out.shape[1])
        far, far_odd = kept(row == 3, factor(6)), kept(row == 3, jnp.where(low, factor(5), factor(7)))
        near = kept(jnp.logical_not(low), factor(1))
        for own, base in ((top, 0), (bottom, half)):
            for start in range(0, half, 16):
                rows, here = slice(base + start, base + start + 16), slice(start, start + 16)
                attention_sum = (
                    own[here, cols].astype(F32) + from_left[rows, :].astype(F32) + from_right[rows, :].astype(F32)
                )
                block_out = (tokens[rows, cols].astype(F32) + attention_sum).astype(BF16)
                past = arrived[rows, :].astype(F32) + far * straight[rows, cols].astype(F32)
                past = past + far_odd * crossed[rows, cols].astype(F32)
                past = past + near * same_row[rows, cols].astype(F32)
                out[rows, :] = (factor(0) * block_out.astype(F32) + past).astype(BF16)

    return kernel


def on_device(
    section_input, history, query_weight, key_weight, value_weight, output_weight, mix_weights
):
    token_rows = section_input[0]
    rows, width = token_rows.shape
    half, sizes = rows // 2, (int(width * SPLIT), width - int(width * SPLIT))
    wq, wk, wv, wo = query_weight[0], key_weight[0], value_weight[0], output_weight[0]
    q_width = wq.shape[1]
    table = mix_weights.T
    half_block, block, kv_width = ((half, width), BF16), ((rows, width), BF16), 8 * LANES
    rows_of = lambda first, last: range(first * ROW, last * ROW)
    swap = lambda i: DILATION_STRIDE if i % ROW < DILATION_STRIDE else -DILATION_STRIDE

    normed, early, far = on_chip(
        prologue_kernel, [block] * 3, token_rows, history[0], limit=6,
        scratch=[pltpu.VMEM((rows, width), BF16), pltpu.SemaphoreType.DMA((3,))], spaces=[pltpu.HBM] * 2,
    )
    left, right = around(normed, 1), around(normed, -1)
    opposite_top, opposite_bottom = around(left[:half], 1), around(right[half:], -1)

    pieces_of = [((rows, size), BF16) for size in sizes]
    late, far_straight, two_straight, one_straight, same_row = on_chip(
        slots_kernel, [block] * 5, history[0],
        limit=6, scratch=[pltpu.SemaphoreType.DMA((5,))], spaces=[pltpu.HBM],
    )
    crossed_early = sent(early, rows_of(0, 3), swap)
    far_odd = sent(far, rows_of(0, 1), lambda i: 3 * ROW + swap(i))
    crossed_late = sent(late, rows_of(0, 2), swap)
    far_even = sent(far_straight, rows_of(0, 1), lambda i: 3 * ROW)

    two_rows = on_chip(two_rows_kernel, pieces_of, table, two_straight, crossed_early, limit=6)
    carried = [sent(piece, rows_of(0, 2), lambda i: ROW) for piece in two_rows]
    near_row = sent(same_row, [i for i in rows_of(0, 4) if swap(i) > 0], swap)
    arrived = []
    for c, piece in enumerate(pieces_of):
        (summed,) = on_chip(
            one_row(sum(sizes[:c])), [piece],
            table, one_straight, crossed_early, crossed_late, carried[c], limit=6,
        )
        arrived.append(sent(summed, rows_of(0, 3), lambda i: ROW))

    (joined,) = on_chip(
        load_kernel, [((width, 2 * LANES), BF16)], wk, wv,
        limit=3, scratch=[pltpu.SemaphoreType.DMA((2,))], spaces=[pltpu.HBM] * 2,
    )
    q0, kv0 = on_chip(
        project_kernel, [((rows, q_width), BF16), ((rows, kv_width), BF16)], normed, wq, joined,
        limit=12,
    )
    q1, kv1 = on_chip(
        project_kernel, [((2 * rows, q_width), BF16), ((2 * rows, kv_width), BF16)],
        left, right, wq, joined, limit=16,
    )
    out3_top, out3_bottom, kv3 = on_chip(
        opposite_kernel, [half_block, half_block, ((rows, kv_width), BF16)],
        opposite_top, opposite_bottom, wq, joined, kv0, kv1, wo,
    )
    from_left_merge, from_right_merge = around(out3_top, 1), around(out3_bottom, -1)
    left_out_top, left_out_bottom, right_out_top, right_out_bottom = on_chip(
        sides_kernel, [half_block] * 4, q1, kv0, kv1, kv3, wo
    )
    own_top, own_bottom = on_chip(own_kernel, [half_block] * 2, q0, kv0, kv1, kv3, wo)
    merged = on_chip(
        merge_kernel, [((rows, size), BF16) for size in 2 * sizes],
        right_out_top, right_out_bottom, left_out_top, left_out_bottom, from_left_merge, from_right_merge, limit=8,
    )
    pieces = []
    for c, size in enumerate(sizes):
        from_left = around(merged[c], 1)
        from_right = around(merged[len(sizes) + c], -1)
        (mixed,) = on_chip(
            finish(sum(sizes[:c])), [((rows, size), BF16)], table, token_rows, own_top, own_bottom,
            from_left, from_right, arrived[c], far_even, far_odd, near_row, limit=8,
        )
        pieces.append(to_next_section(mixed))
    return jnp.concatenate(pieces, axis=1)[None]


def solution(mesh):
    placed = (
        P("section", "tensor", None),
        P("section", None, "tensor", None),
        P("section", None, "tensor"),
        P("section", None, "tensor"),
        P("section", None, "tensor"),
        P("section", "tensor", None),
        P(),
    )

    return jax.shard_map(
        on_device,
        mesh=mesh,
        in_specs=placed,
        out_specs=P("section", "tensor", None),
        check_vma=False,
    )
```

time: 116 us -> 114 us (0.983)
  Pallas kernels: 27.2 us -> 23.1 us
    ppermute x10, waiting for transfers between devices: 21.4 us -> 14.6 us  [around(): lax.ppermute(value, 'tensor', [(i, (i + steps) % count) for i in range(co...]
    ppermute x7 -> x9, waiting for transfers between devices: 12 us -> 16.9 us  [sent(): return lax.ppermute(value, 'section', [(i, i + steps(i)) for i in sources])]
    pallas_call x15 -> x14, Pallas kernels: 27.2 us -> 23.1 us  [on_chip(): pl.pallas_call(body, out_shape=[pltpu.VMEM(shape, dtype) for shape, dtype...]
    ppermute x2, waiting for transfers between devices: 11.9 us -> 14.6 us  [to_next_section(): lax.ppermute(block, 'section', [(i, (i + 1) % count) for i in range(count)])]
    ppermute x7 -> x9, starting transfers between devices: 24.9 us -> 26.6 us  [sent(): return lax.ppermute(value, 'section', [(i, i + steps(i)) for i in sources])]
  transfers between devices with their start and end apart: 19 -> 21, of which waited for: 6 -> 9; matrix products, arithmetic and copies ran while one was open for 0% -> 0% of each run, Pallas kernels for 22% -> 19%
where the time goes in v1:
time: 114 us
  waiting for transfers between devices  46.1 us (40%)
  starting transfers between devices  42.7 us (37%)
  Pallas kernels  23.1 us (20%)
    ppermute x9, starting transfers between devices, sent(): return lax.ppermute(value, 'section', [(i, i + steps(i)) for i in sources])  26.6 us
    pallas_call x14, Pallas kernels, on_chip(): pl.pallas_call(body, out_shape=[pltpu.VMEM(shape, dtype) for shape, dtype...  23.1 us
    ppermute x9, waiting for transfers between devices, sent(): return lax.ppermute(value, 'section', [(i, i + steps(i)) for i in sources])  16.9 us
    ppermute x10, starting transfers between devices, around(): lax.ppermute(value, 'tensor', [(i, (i + steps) % count) for i in range(co...  15.9 us
    ppermute x2, waiting for transfers between devices, to_next_section(): lax.ppermute(block, 'section', [(i, (i + 1) % count) for i in range(count)])  14.6 us
    ppermute x10, waiting for transfers between devices, around(): lax.ppermute(value, 'tensor', [(i, (i + steps) % count) for i in range(co...  14.6 us
  transfers between devices with their start and end apart: 21, of which 9 were waited for; matrix products, arithmetic and copies ran while one was open for 0% of the time, Pallas kernels for 19%

profile of v1, /device:TPU:0, one launch (start us, length us, event | category | flops | bytes accessed | tf_op | source)
XLA Modules:
  0.0 113.5 jit_solution(6948508124279816570)
XLA Ops:
  0.0 1.9 %shard_map.73 = (bf16[128,4096]{1,0:T(8,128)(2,1)S(1)}, bf16[128,4096]{1,0:T(8,128)(2,1)S(1)}, bf16[128,4096]{1,0:T(8,128)(2,1)S(1)}) custom-call(bf16[128,4096]{1,0:T(8,128)(2,1)} %bitcast.19, bf16[7,128,4096]{2,1,0:T(8,128)(2,1)} %bitcast.27), custom_call_target="tpu_custom_call" | custom-call | tf_op jit(solution)/shard_map/pallas_call | solution.py:41
  1.9 2.9 %collective-permute-start.1 = (bf16[128,4096]{1,0:T(8,128)(2,1)S(1)}, bf16[128,4096]{1,0:T(8,128)(2,1)S(1)}, u32[]{:S(2)}, u32[]{:S(2)}) collective-permute-start(bf16[128,4096]{1,0:T(8,128)(2,1)S(1)} %get-tuple-element.32.refs_0_), channel_id=1, source_target_pairs={{0,3},{1,0},{2,1},{3,2},{4,7},{5,4},{6,5},{7,6},{8,11},{9,8},{10,9... | collective-permute-start | bytes 3145736 | tf_op jit(solution)/shard_map/ppermute | solution.py:23
  4.8 5.8 %collective-permute-start.8 = (bf16[128,4096]{1,0:T(8,128)(2,1)S(1)}, bf16[128,4096]{1,0:T(8,128)(2,1)S(1)}, u32[]{:S(2)}, u32[]{:S(2)}) collective-permute-start(bf16[128,4096]{1,0:T(8,128)(2,1)S(1)} %get-tuple-element.49), channel_id=1, source_target_pairs={{0,16},{4,20},{8,24},{12,28},{16,0},{20,4},{24,8},{28,12},{32,48},... | collective-permute-start | bytes 3145736 | tf_op jit(solution)/shard_map/ppermute | solution.py:27
  10.6 0.0 slice-start
  10.6 2.7 %shard_map.81 = (bf16[128,4096]{1,0:T(8,128)(2,1)S(1)}, bf16[128,4096]{1,0:T(8,128)(2,1)S(1)}, bf16[128,4096]{1,0:T(8,128)(2,1)S(1)}, bf16[128,4096]{1,0:T(8,128)(2,1)S(1)}, bf16[128,4096]{1,0:T(8,128)(2,1)S(1)}) custom-call(bf16[7,128,4096]{2,1,0:T(8,128)(2,1)} %bitcast.28), custom_call_target="tpu_custom_call" | custom-call | tf_op jit(solution)/shard_map/pallas_call | solution.py:41
  13.3 0.0 slice-start.1
  13.4 2.1 %collective-permute-start.9 = (bf16[128,4096]{1,0:T(8,128)(2,1)S(1)}, bf16[128,4096]{1,0:T(8,128)(2,1)S(1)}, u32[]{:S(2)}, u32[]{:S(2)}) collective-permute-start(bf16[128,4096]{1,0:T(8,128)(2,1)S(1)} %get-tuple-element.50), channel_id=1, source_target_pairs={{0,16},{4,20},{8,24},{12,28},{16,0},{20,4},{24,8},{28,12},{32,48},... | collective-permute-start | bytes 3145736 | tf_op jit(solution)/shard_map/ppermute | solution.py:27
  15.4 11.8 %collective-permute-done.1.refs_1_ = bf16[128,4096]{1,0:T(8,128)(2,1)S(1)} collective-permute-done((bf16[128,4096]{1,0:T(8,128)(2,1)S(1)}, bf16[128,4096]{1,0:T(8,128)(2,1)S(1)}, u32[]{:S(2)}, u32[]{:S(2)}) %collective-permute-start.1) | collective-permute-done | bytes 1048608 | tf_op jit(solution)/shard_map/ppermute | solution.py:23
  27.3 3.8 %collective-permute-start.3 = (bf16[64,4096]{1,0:T(8,128)(2,1)S(1)}, bf16[64,4096]{1,0:T(8,128)(2,1)S(1)}, u32[]{:S(2)}, u32[]{:S(2)}) collective-permute-start(bf16[64,4096]{1,0:T(8,128)(2,1)S(1)} %slice.9), channel_id=1, source_target_pairs={{0,3},{1,0},{2,1},{3,2},{4,7},{5,4},{6,5},{7,6},{8,11},{9,8},{10,9... | collective-permute-start | bytes 1572872 | tf_op jit(solution)/shard_map/ppermute | solution.py:23
  31.1 0.1 collective-permute-start.2
  31.2 3.4 %collective-permute-done.8.crossed.crossed_early = bf16[128,4096]{1,0:T(8,128)(2,1)S(1)} collective-permute-done((bf16[128,4096]{1,0:T(8,128)(2,1)S(1)}, bf16[128,4096]{1,0:T(8,128)(2,1)S(1)}, u32[]{:S(2)}, u32[]{:S(2)}) %collective-permute-start.8) | collective-permute-done | bytes 1048608 | tf_op jit(solution)/shard_map/ppermute | solution.py:27
  34.6 0.5 shard_map.82
  35.1 3.5 %collective-permute-start.10 = (bf16[128,2560]{1,0:T(8,128)(2,1)S(1)}, bf16[128,2560]{1,0:T(8,128)(2,1)S(1)}, u32[]{:S(2)}, u32[]{:S(2)}) collective-permute-start(bf16[128,2560]{1,0:T(8,128)(2,1)S(1)} %get-tuple-element.52), channel_id=1, source_target_pairs={{0,32},{4,36},{8,40},{12,44},{16,48},{20,52},{24,56},{28,60},{32,6... | collective-permute-start | bytes 1966088 | tf_op jit(solution)/shard_map/ppermute | solution.py:27
  38.6 2.1 %collective-permute-start.13 = (bf16[128,4096]{1,0:T(8,128)(2,1)S(1)}, bf16[128,4096]{1,0:T(8,128)(2,1)S(1)}, u32[]{:S(2)}, u32[]{:S(2)}) collective-permute-start(bf16[128,4096]{1,0:T(8,128)(2,1)S(1)} %get-tuple-element.54), channel_id=1, source_target_pairs={{0,112},{4,116},{8,120},{12,124},{16,96},{20,100},{24,104},{28,108... | collective-permute-start | bytes 3145736 | tf_op jit(solution)/shard_map/ppermute | solution.py:27
  40.7 1.6 %shard_map.74.refs_2_.refs_3_.joined = bf16[4096,256]{1,0:T(8,128)(2,1)S(1)} custom-call(bf16[4096,128]{1,0:T(8,128)(2,1)} %bitcast.29, bf16[4096,128]{1,0:T(8,128)(2,1)} %bitcast.30), custom_call_target="tpu_custom_call" | custom-call | tf_op jit(solution)/shard_map/pallas_call | solution.py:41
  42.3 0.0 slice-start.2
  42.3 1.3 %shard_map.75 = (bf16[128,768]{1,0:T(8,128)(2,1)S(1)}, bf16[128,1024]{1,0:T(8,128)(2,1)S(1)}) custom-call(bf16[128,4096]{1,0:T(8,128)(2,1)S(1)} %get-tuple-element.32.refs_0_, bf16[4096,768]{1,0:T(8,128)(2,1)S(1)} %bitcast.11, bf16[4096,256]{1,0:T(8,128)(2,1)S(1)} %shard_map.74.refs_2_.refs_3_.joined), custom_call_target="tpu_custom_call" | custom-call | tf_op jit(solution)/shard_map/pallas_call | solution.py:41
  43.7 0.0 slice-start.3
  43.7 2.4 %shard_map.76 = (bf16[256,768]{1,0:T(8,128)(2,1)S(1)}, bf16[256,1024]{1,0:T(8,128)(2,1)S(1)}) custom-call(bf16[128,4096]{1,0:T(8,128)(2,1)S(1)} %collective-permute-done.refs_0_, bf16[128,4096]{1,0:T(8,128)(2,1)S(1)} %collective-permute-done.1.refs_1_, bf16[4096,768]{1,0:T(8,128)(2,1)S(1)} %bitcast.12, bf16[4096,256]{1,0:T(8,128)(2,1)S(1)} %shard_map.74.refs_2_.refs_3_.joined), custom_call_target="tpu_custom_call" | custom-call | tf_op jit(solution)/shard_map/pallas_call | solution.py:41
  46.1 3.4 %shard_map.77 = (bf16[64,4096]{1,0:T(8,128)(2,1)S(1)}, bf16[64,4096]{1,0:T(8,128)(2,1)S(1)}, bf16[128,1024]{1,0:T(8,128)(2,1)S(1)}) custom-call(bf16[64,4096]{1,0:T(8,128)(2,1)S(1)} %collective-permute-done.2.top, bf16[64,4096]{1,0:T(8,128)(2,1)S(1)} %collective-permute-done.3.bottom, bf16[4096,768]{1,0:T(8,128)(2,1)S(1)} %bitcast.13, ...), custom_call_target="tpu_custom_call" | custom-call | tf_op jit(solution)/shard_map/pallas_call | solution.py:41
  49.6 0.1 collective-permute-start.4
  49.7 3.2 %collective-permute-start.5 = (bf16[64,4096]{1,0:T(8,128)(2,1)S(1)}, bf16[64,4096]{1,0:T(8,128)(2,1)S(1)}, u32[]{:S(2)}, u32[]{:S(2)}) collective-permute-start(bf16[64,4096]{1,0:T(8,128)(2,1)S(1)} %get-tuple-element.45), channel_id=1, source_target_pairs={{0,3},{1,0},{2,1},{3,2},{4,7},{5,4},{6,5},{7,6},{8,11},{9,8},{10,9... | collective-permute-start | bytes 1572872 | tf_op jit(solution)/shard_map/ppermute | solution.py:23
  52.9 3.0 %collective-permute-done.9.crossed_late = bf16[128,4096]{1,0:T(8,128)(2,1)S(1)} collective-permute-done((bf16[128,4096]{1,0:T(8,128)(2,1)S(1)}, bf16[128,4096]{1,0:T(8,128)(2,1)S(1)}, u32[]{:S(2)}, u32[]{:S(2)}) %collective-permute-start.9) | collective-permute-done | bytes 1048608 | tf_op jit(solution)/shard_map/ppermute | solution.py:27
  55.9 1.3 %collective-permute-start.12 = (bf16[128,4096]{1,0:T(8,128)(2,1)S(1)}, bf16[128,4096]{1,0:T(8,128)(2,1)S(1)}, u32[]{:S(2)}, u32[]{:S(2)}) collective-permute-start(bf16[128,4096]{1,0:T(8,128)(2,1)S(1)} %get-tuple-element.53), channel_id=1, source_target_pairs={{0,96},{4,100},{8,104},{12,108},{16,112},{20,116},{24,120},{28,124... | collective-permute-start | bytes 3145736 | tf_op jit(solution)/shard_map/ppermute | solution.py:27
  57.3 5.2 %collective-permute-start.14 = (bf16[128,4096]{1,0:T(8,128)(2,1)S(1)}, bf16[128,4096]{1,0:T(8,128)(2,1)S(1)}, u32[]{:S(2)}, u32[]{:S(2)}) collective-permute-start(bf16[128,4096]{1,0:T(8,128)(2,1)S(1)} %get-tuple-element.55), channel_id=1, source_target_pairs={{0,16},{4,20},{8,24},{12,28},{32,48},{36,52},{40,56},{44,60},{64,8... | collective-permute-start | bytes 3145736 | tf_op jit(solution)/shard_map/ppermute | solution.py:27
  62.5 0.6 collective-permute-done.4.from_left
  63.1 2.3 %collective-permute-start.18 = (bf16[128,1536]{1,0:T(8,128)(2,1)S(1)}, bf16[128,1536]{1,0:T(8,128)(2,1)S(1)}, u32[]{:S(2)}, u32[]{:S(2)}) collective-permute-start(bf16[128,1536]{1,0:T(8,128)(2,1)S(1)} %get-tuple-element.58), channel_id=1, source_target_pairs={{0,32},{4,36},{8,40},{12,44},{16,48},{20,52},{24,56},{28,60},{32,6... | collective-permute-start | bytes 1179656 | tf_op jit(solution)/shard_map/ppermute | solution.py:27
  65.4 0.6 shard_map.83
  66.0 3.0 %collective-permute-start.11 = (bf16[128,2560]{1,0:T(8,128)(2,1)S(1)}, bf16[128,2560]{1,0:T(8,128)(2,1)S(1)}, u32[]{:S(2)}, u32[]{:S(2)}) collective-permute-start(bf16[128,2560]{1,0:T(8,128)(2,1)S(1)} %shard_map.83), channel_id=1, source_target_pairs={{0,32},{4,36},{8,40},{12,44},{16,48},{20,52},{24,56},{28,60},{32,6... | collective-permute-start | bytes 1966088 | tf_op jit(solution)/shard_map/ppermute | solution.py:27
  69.1 4.2 %shard_map.79 = (bf16[64,4096]{1,0:T(8,128)(2,1)S(1)}, bf16[64,4096]{1,0:T(8,128)(2,1)S(1)}, bf16[64,4096]{1,0:T(8,128)(2,1)S(1)}, bf16[64,4096]{1,0:T(8,128)(2,1)S(1)}) custom-call(bf16[256,768]{1,0:T(8,128)(2,1)S(1)} %get-tuple-element.39.query, bf16[128,1024]{1,0:T(8,128)(2,1)S(1)} %get-tuple-element.34.kv0, bf16[256,1024]{1,0:T(8,128)(2,1)S(1)} %get-tuple-element.35.kv1, ...), custom_call_target="tpu_custom_call" | custom-call | tf_op jit(solution)/shard_map/pallas_call | solution.py:41
  73.3 0.3 shard_map.80
  73.6 0.1 collective-permute-start.6
  73.7 1.2 %collective-permute-done.18.carried = bf16[128,1536]{1,0:T(8,128)(2,1)S(1)} collective-permute-done((bf16[128,1536]{1,0:T(8,128)(2,1)S(1)}, bf16[128,1536]{1,0:T(8,128)(2,1)S(1)}, u32[]{:S(2)}, u32[]{:S(2)}) %collective-permute-start.18) | collective-permute-done | bytes 393248 | tf_op jit(solution)/shard_map/ppermute | solution.py:27
  74.9 3.0 %collective-permute-start.7 = (bf16[128,2560]{1,0:T(8,128)(2,1)S(1)}, bf16[128,2560]{1,0:T(8,128)(2,1)S(1)}, u32[]{:S(2)}, u32[]{:S(2)}) collective-permute-start(bf16[128,2560]{1,0:T(8,128)(2,1)S(1)} %get-tuple-element.47), channel_id=1, source_target_pairs={{0,3},{1,0},{2,1},{3,2},{4,7},{5,4},{6,5},{7,6},{8,11},{9,8},{10,9... | collective-permute-start | bytes 1966088 | tf_op jit(solution)/shard_map/ppermute | solution.py:23
  77.8 0.4 shard_map.85
  78.2 6.2 %collective-permute-done.12.straight = bf16[128,4096]{1,0:T(8,128)(2,1)S(1)} collective-permute-done((bf16[128,4096]{1,0:T(8,128)(2,1)S(1)}, bf16[128,4096]{1,0:T(8,128)(2,1)S(1)}, u32[]{:S(2)}, u32[]{:S(2)}) %collective-permute-start.12) | collective-permute-done | bytes 1048608 | tf_op jit(solution)/shard_map/ppermute | solution.py:27
  84.4 1.3 %collective-permute-start.19 = (bf16[128,1536]{1,0:T(8,128)(2,1)S(1)}, bf16[128,1536]{1,0:T(8,128)(2,1)S(1)}, u32[]{:S(2)}, u32[]{:S(2)}) collective-permute-start(bf16[128,1536]{1,0:T(8,128)(2,1)S(1)} %shard_map.85), channel_id=1, source_target_pairs={{0,32},{4,36},{8,40},{12,44},{16,48},{20,52},{24,56},{28,60},{32,6... | collective-permute-start | bytes 1179656 | tf_op jit(solution)/shard_map/ppermute | solution.py:27
  85.7 0.1 collective-permute-start.16
  85.8 3.0 %collective-permute-done.11.arrived = bf16[128,2560]{1,0:T(8,128)(2,1)S(1)} collective-permute-done((bf16[128,2560]{1,0:T(8,128)(2,1)S(1)}, bf16[128,2560]{1,0:T(8,128)(2,1)S(1)}, u32[]{:S(2)}, u32[]{:S(2)}) %collective-permute-start.11) | collective-permute-done | bytes 655392 | tf_op jit(solution)/shard_map/ppermute | solution.py:27
  88.8 2.7 %collective-permute-start.17 = (bf16[128,1536]{1,0:T(8,128)(2,1)S(1)}, bf16[128,1536]{1,0:T(8,128)(2,1)S(1)}, u32[]{:S(2)}, u32[]{:S(2)}) collective-permute-start(bf16[128,1536]{1,0:T(8,128)(2,1)S(1)} %get-tuple-element.57), channel_id=1, source_target_pairs={{0,3},{1,0},{2,1},{3,2},{4,7},{5,4},{6,5},{7,6},{8,11},{9,8},{10,9... | collective-permute-start | bytes 1179656 | tf_op jit(solution)/shard_map/ppermute | solution.py:23
  91.5 2.2 %shard_map.78 = (bf16[64,4096]{1,0:T(8,128)(2,1)S(1)}, bf16[64,4096]{1,0:T(8,128)(2,1)S(1)}) custom-call(bf16[128,768]{1,0:T(8,128)(2,1)S(1)} %get-tuple-element.33.query, bf16[128,1024]{1,0:T(8,128)(2,1)S(1)} %get-tuple-element.34.kv0, bf16[256,1024]{1,0:T(8,128)(2,1)S(1)} %get-tuple-element.35.kv1, bf16[128,1024]{1,0:T(8,128)(2,1)S(1)} %get-tuple-element.36.kv3, ...), custom_call_target="tpu_custom_call" | custom-call | tf_op jit(solution)/shard_map/pallas_call | solution.py:41
  93.8 1.0 shard_map.84
  94.8 0.1 collective-permute-start.15
  94.9 2.2 %collective-permute-done.16.from_left = bf16[128,1536]{1,0:T(8,128)(2,1)S(1)} collective-permute-done((bf16[128,1536]{1,0:T(8,128)(2,1)S(1)}, bf16[128,1536]{1,0:T(8,128)(2,1)S(1)}, u32[]{:S(2)}, u32[]{:S(2)}) %collective-permute-start.16) | collective-permute-done | bytes 393248 | tf_op jit(solution)/shard_map/ppermute | solution.py:23
  97.2 0.6 shard_map.86
  97.8 0.1 collective-permute-start.20
  97.8 14.6 %collective-permute-done.20 = bf16[128,1536]{1,0:T(8,128)(2,1)S(1)} collective-permute-done((bf16[128,1536]{1,0:T(8,128)(2,1)S(1)}, bf16[128,1536]{1,0:T(8,128)(2,1)S(1)}, u32[]{:S(2)}, u32[]{:S(2)}) %collective-permute-start.20) | collective-permute-done | bytes 393248 | tf_op jit(solution)/shard_map/ppermute | solution.py:32
  112.5 1.1 maximum_bitcast_fusion
  (25 shorter events, 0.1 us)
Async XLA Ops:
  1.9 25.4 %collective-permute-start.1 = (bf16[128,4096]{1,0:T(8,128)(2,1)S(1)}, bf16[128,4096]{1,0:T(8,128)(2,1)S(1)}, u32[]{:S(2)}, u32[]{:S(2)}) collective-permute-start(bf16[128,4096]{1,0:T(8,128)(2,1)S(1)} %get-tuple-element.32.refs_0_), channel_id=1, source_target_pairs={{0,3},{1,0},{2,1},{3,2},{4,7},{5,4},{6,5},{7,6},{8,11},{9,8},{10,9... | collective-permute-start | bytes 3145736 | tf_op jit(solution)/shard_map/ppermute | solution.py:23
  4.8 26.2 %collective-permute-start = (bf16[128,4096]{1,0:T(8,128)(2,1)S(1)}, bf16[128,4096]{1,0:T(8,128)(2,1)S(1)}, u32[]{:S(2)}, u32[]{:S(2)}) collective-permute-start(bf16[128,4096]{1,0:T(8,128)(2,1)S(1)} %get-tuple-element.32.refs_0_), channel_id=1, source_target_pairs={{0,1},{1,2},{2,3},{3,0},{4,5},{5,6},{6,7},{7,4},{8,9},{9,10},{10,1... | collective-permute-start | bytes 3145736 | tf_op jit(solution)/shard_map/ppermute | solution.py:23
  4.8 29.8 %collective-permute-start.8 = (bf16[128,4096]{1,0:T(8,128)(2,1)S(1)}, bf16[128,4096]{1,0:T(8,128)(2,1)S(1)}, u32[]{:S(2)}, u32[]{:S(2)}) collective-permute-start(bf16[128,4096]{1,0:T(8,128)(2,1)S(1)} %get-tuple-element.49), channel_id=1, source_target_pairs={{0,16},{4,20},{8,24},{12,28},{16,0},{20,4},{24,8},{28,12},{32,48},... | collective-permute-start | bytes 3145736 | tf_op jit(solution)/shard_map/ppermute | solution.py:27
  10.6 31.7 %slice-start = ((s8[6291456]{0:T(1024)(128)(4,1)}), s8[4194304]{0:T(1024)(128)(4,1)S(1)}, s32[]{:S(2)}) async-start(s8[6291456]{0:T(1024)(128)(4,1)} %bitcast.9), calls=%async_computation | async-start | bytes 8388608
  13.3 21.3 %copy-start.1 = (f32[32,8]{0,1:T(8,128)S(1)}, f32[32,8]{0,1:T(8,128)}, u32[]{:S(2)}) copy-start(f32[32,8]{0,1:T(8,128)} %param.13) | copy-start | bytes 3076
  13.3 28.9 %slice-start.1 = ((s8[6291456]{0:T(1024)(128)(4,1)}), s8[2097152]{0:T(1024)(128)(4,1)S(1)}, s32[]{:S(2)}) async-start(s8[6291456]{0:T(1024)(128)(4,1)} %bitcast.9), calls=%async_computation.1 | async-start | bytes 4194304
  13.4 42.6 %collective-permute-start.9 = (bf16[128,4096]{1,0:T(8,128)(2,1)S(1)}, bf16[128,4096]{1,0:T(8,128)(2,1)S(1)}, u32[]{:S(2)}, u32[]{:S(2)}) collective-permute-start(bf16[128,4096]{1,0:T(8,128)(2,1)S(1)} %get-tuple-element.50), channel_id=1, source_target_pairs={{0,16},{4,20},{8,24},{12,28},{16,0},{20,4},{24,8},{28,12},{32,48},... | collective-permute-start | bytes 3145736 | tf_op jit(solution)/shard_map/ppermute | solution.py:27
  27.3 18.8 %collective-permute-start.3 = (bf16[64,4096]{1,0:T(8,128)(2,1)S(1)}, bf16[64,4096]{1,0:T(8,128)(2,1)S(1)}, u32[]{:S(2)}, u32[]{:S(2)}) collective-permute-start(bf16[64,4096]{1,0:T(8,128)(2,1)S(1)} %slice.9), channel_id=1, source_target_pairs={{0,3},{1,0},{2,1},{3,2},{4,7},{5,4},{6,5},{7,6},{8,11},{9,8},{10,9... | collective-permute-start | bytes 1572872 | tf_op jit(solution)/shard_map/ppermute | solution.py:23
  31.1 15.0 %collective-permute-start.2 = (bf16[64,4096]{1,0:T(8,128)(2,1)S(1)}, bf16[64,4096]{1,0:T(8,128)(2,1)S(1)}, u32[]{:S(2)}, u32[]{:S(2)}) collective-permute-start(bf16[64,4096]{1,0:T(8,128)(2,1)S(1)} %slice.8), channel_id=1, source_target_pairs={{0,1},{1,2},{2,3},{3,0},{4,5},{5,6},{6,7},{7,4},{8,9},{9,10},{10,1... | collective-permute-start | bytes 1572872 | tf_op jit(solution)/shard_map/ppermute | solution.py:23
  35.1 22.2 %collective-permute-start.10 = (bf16[128,2560]{1,0:T(8,128)(2,1)S(1)}, bf16[128,2560]{1,0:T(8,128)(2,1)S(1)}, u32[]{:S(2)}, u32[]{:S(2)}) collective-permute-start(bf16[128,2560]{1,0:T(8,128)(2,1)S(1)} %get-tuple-element.52), channel_id=1, source_target_pairs={{0,32},{4,36},{8,40},{12,44},{16,48},{20,52},{24,56},{28,60},{32,6... | collective-permute-start | bytes 1966088 | tf_op jit(solution)/shard_map/ppermute | solution.py:27
  38.6 35.0 %collective-permute-start.13 = (bf16[128,4096]{1,0:T(8,128)(2,1)S(1)}, bf16[128,4096]{1,0:T(8,128)(2,1)S(1)}, u32[]{:S(2)}, u32[]{:S(2)}) collective-permute-start(bf16[128,4096]{1,0:T(8,128)(2,1)S(1)} %get-tuple-element.54), channel_id=1, source_target_pairs={{0,112},{4,116},{8,120},{12,124},{16,96},{20,100},{24,104},{28,108... | collective-permute-start | bytes 3145736 | tf_op jit(solution)/shard_map/ppermute | solution.py:27
  42.3 3.8 %slice-start.2 = ((s8[6291456]{0:T(1024)(128)(4,1)}), s8[4194304]{0:T(1024)(128)(4,1)S(1)}, s32[]{:S(2)}) async-start(s8[6291456]{0:T(1024)(128)(4,1)} %bitcast.14), calls=%async_computation.2 | async-start | bytes 8388608
  43.7 2.5 %slice-start.3 = ((s8[6291456]{0:T(1024)(128)(4,1)}), s8[2097152]{0:T(1024)(128)(4,1)S(1)}, s32[]{:S(2)}) async-start(s8[6291456]{0:T(1024)(128)(4,1)} %bitcast.14), calls=%async_computation.3 | async-start | bytes 4194304
  49.6 13.5 %collective-permute-start.4 = (bf16[64,4096]{1,0:T(8,128)(2,1)S(1)}, bf16[64,4096]{1,0:T(8,128)(2,1)S(1)}, u32[]{:S(2)}, u32[]{:S(2)}) collective-permute-start(bf16[64,4096]{1,0:T(8,128)(2,1)S(1)} %get-tuple-element.44), channel_id=1, source_target_pairs={{0,1},{1,2},{2,3},{3,0},{4,5},{5,6},{6,7},{7,4},{8,9},{9,10},{10,1... | collective-permute-start | bytes 1572872 | tf_op jit(solution)/shard_map/ppermute | solution.py:23
  49.7 16.3 %collective-permute-start.5 = (bf16[64,4096]{1,0:T(8,128)(2,1)S(1)}, bf16[64,4096]{1,0:T(8,128)(2,1)S(1)}, u32[]{:S(2)}, u32[]{:S(2)}) collective-permute-start(bf16[64,4096]{1,0:T(8,128)(2,1)S(1)} %get-tuple-element.45), channel_id=1, source_target_pairs={{0,3},{1,0},{2,1},{3,2},{4,7},{5,4},{6,5},{7,6},{8,11},{9,8},{10,9... | collective-permute-start | bytes 1572872 | tf_op jit(solution)/shard_map/ppermute | solution.py:23
  55.9 28.5 %collective-permute-start.12 = (bf16[128,4096]{1,0:T(8,128)(2,1)S(1)}, bf16[128,4096]{1,0:T(8,128)(2,1)S(1)}, u32[]{:S(2)}, u32[]{:S(2)}) collective-permute-start(bf16[128,4096]{1,0:T(8,128)(2,1)S(1)} %get-tuple-element.53), channel_id=1, source_target_pairs={{0,96},{4,100},{8,104},{12,108},{16,112},{20,116},{24,120},{28,124... | collective-permute-start | bytes 3145736 | tf_op jit(solution)/shard_map/ppermute | solution.py:27
  57.3 28.4 %collective-permute-start.14 = (bf16[128,4096]{1,0:T(8,128)(2,1)S(1)}, bf16[128,4096]{1,0:T(8,128)(2,1)S(1)}, u32[]{:S(2)}, u32[]{:S(2)}) collective-permute-start(bf16[128,4096]{1,0:T(8,128)(2,1)S(1)} %get-tuple-element.55), channel_id=1, source_target_pairs={{0,16},{4,20},{8,24},{12,28},{32,48},{36,52},{40,56},{44,60},{64,8... | collective-permute-start | bytes 3145736 | tf_op jit(solution)/shard_map/ppermute | solution.py:27
  63.1 11.8 %collective-permute-start.18 = (bf16[128,1536]{1,0:T(8,128)(2,1)S(1)}, bf16[128,1536]{1,0:T(8,128)(2,1)S(1)}, u32[]{:S(2)}, u32[]{:S(2)}) collective-permute-start(bf16[128,1536]{1,0:T(8,128)(2,1)S(1)} %get-tuple-element.58), channel_id=1, source_target_pairs={{0,32},{4,36},{8,40},{12,44},{16,48},{20,52},{24,56},{28,60},{32,6... | collective-permute-start | bytes 1179656 | tf_op jit(solution)/shard_map/ppermute | solution.py:27
  66.0 22.8 %collective-permute-start.11 = (bf16[128,2560]{1,0:T(8,128)(2,1)S(1)}, bf16[128,2560]{1,0:T(8,128)(2,1)S(1)}, u32[]{:S(2)}, u32[]{:S(2)}) collective-permute-start(bf16[128,2560]{1,0:T(8,128)(2,1)S(1)} %shard_map.83), channel_id=1, source_target_pairs={{0,32},{4,36},{8,40},{12,44},{16,48},{20,52},{24,56},{28,60},{32,6... | collective-permute-start | bytes 1966088 | tf_op jit(solution)/shard_map/ppermute | solution.py:27
  73.6 20.2 %collective-permute-start.6 = (bf16[128,2560]{1,0:T(8,128)(2,1)S(1)}, bf16[128,2560]{1,0:T(8,128)(2,1)S(1)}, u32[]{:S(2)}, u32[]{:S(2)}) collective-permute-start(bf16[128,2560]{1,0:T(8,128)(2,1)S(1)} %get-tuple-element.46), channel_id=1, source_target_pairs={{0,1},{1,2},{2,3},{3,0},{4,5},{5,6},{6,7},{7,4},{8,9},{9,10},{10,1... | collective-permute-start | bytes 1966088 | tf_op jit(solution)/shard_map/ppermute | solution.py:23
  74.9 18.9 %collective-permute-start.7 = (bf16[128,2560]{1,0:T(8,128)(2,1)S(1)}, bf16[128,2560]{1,0:T(8,128)(2,1)S(1)}, u32[]{:S(2)}, u32[]{:S(2)}) collective-permute-start(bf16[128,2560]{1,0:T(8,128)(2,1)S(1)} %get-tuple-element.47), channel_id=1, source_target_pairs={{0,3},{1,0},{2,1},{3,2},{4,7},{5,4},{6,5},{7,6},{8,11},{9,8},{10,9... | collective-permute-start | bytes 1966088 | tf_op jit(solution)/shard_map/ppermute | solution.py:23
  84.4 10.5 %collective-permute-start.19 = (bf16[128,1536]{1,0:T(8,128)(2,1)S(1)}, bf16[128,1536]{1,0:T(8,128)(2,1)S(1)}, u32[]{:S(2)}, u32[]{:S(2)}) collective-permute-start(bf16[128,1536]{1,0:T(8,128)(2,1)S(1)} %shard_map.85), channel_id=1, source_target_pairs={{0,32},{4,36},{8,40},{12,44},{16,48},{20,52},{24,56},{28,60},{32,6... | collective-permute-start | bytes 1179656 | tf_op jit(solution)/shard_map/ppermute | solution.py:27
  85.7 11.4 %collective-permute-start.16 = (bf16[128,1536]{1,0:T(8,128)(2,1)S(1)}, bf16[128,1536]{1,0:T(8,128)(2,1)S(1)}, u32[]{:S(2)}, u32[]{:S(2)}) collective-permute-start(bf16[128,1536]{1,0:T(8,128)(2,1)S(1)} %get-tuple-element.56), channel_id=1, source_target_pairs={{0,1},{1,2},{2,3},{3,0},{4,5},{5,6},{6,7},{7,4},{8,9},{9,10},{10,1... | collective-permute-start | bytes 1179656 | tf_op jit(solution)/shard_map/ppermute | solution.py:23
  88.8 8.3 %collective-permute-start.17 = (bf16[128,1536]{1,0:T(8,128)(2,1)S(1)}, bf16[128,1536]{1,0:T(8,128)(2,1)S(1)}, u32[]{:S(2)}, u32[]{:S(2)}) collective-permute-start(bf16[128,1536]{1,0:T(8,128)(2,1)S(1)} %get-tuple-element.57), channel_id=1, source_target_pairs={{0,3},{1,0},{2,1},{3,2},{4,7},{5,4},{6,5},{7,6},{8,11},{9,8},{10,9... | collective-permute-start | bytes 1179656 | tf_op jit(solution)/shard_map/ppermute | solution.py:23
  91.5 2.3 %copy-start = (bf16[1,128,4096]{2,1,0:T(8,128)(2,1)S(1)}, bf16[1,128,4096]{2,1,0:T(8,128)(2,1)}, u32[]{:S(2)}) copy-start(bf16[1,128,4096]{2,1,0:T(8,128)(2,1)} %param.7) | copy-start | bytes 3145732
  94.8 17.6 %collective-permute-start.15 = (bf16[128,2560]{1,0:T(8,128)(2,1)S(1)}, bf16[128,2560]{1,0:T(8,128)(2,1)S(1)}, u32[]{:S(2)}, u32[]{:S(2)}) collective-permute-start(bf16[128,2560]{1,0:T(8,128)(2,1)S(1)} %shard_map.84), channel_id=1, source_target_pairs={{0,4},{4,8},{8,12},{12,16},{16,20},{20,24},{24,28},{28,32},{32,36}... | collective-permute-start | bytes 1966088 | tf_op jit(solution)/shard_map/ppermute | solution.py:32
  97.8 14.7 %collective-permute-start.20 = (bf16[128,1536]{1,0:T(8,128)(2,1)S(1)}, bf16[128,1536]{1,0:T(8,128)(2,1)S(1)}, u32[]{:S(2)}, u32[]{:S(2)}) collective-permute-start(bf16[128,1536]{1,0:T(8,128)(2,1)S(1)} %shard_map.86), channel_id=1, source_target_pairs={{0,4},{4,8},{8,12},{12,16},{16,20},{20,24},{24,28},{28,32},{32,36}... | collective-permute-start | bytes 1179656 | tf_op jit(solution)/shard_map/ppermute | solution.py:32

commit v2 on v1

--- a/solution.py
+++ b/solution.py
@@ -11,7 +11,8 @@
 LOG2_E = 1.4426950408889634
 DILATION_STRIDE = 4
 ROW = 2 * DILATION_STRIDE
-SPLIT = 5 / 8
+CARRIED_PIECES = (5, 3)
+MERGED_PIECES = (5, 5, 6)
 PROJECTED_COLUMNS = 1024
 MIB = 1 << 20
 BF16, F32 = jnp.bfloat16, jnp.float32
@@ -234,40 +235,41 @@
     put_projected(attended(query[...], kv, BLOCK_OFFSETS[0]), outward, top, bottom)
 
 
-def merge_kernel(right_top, right_bottom, left_top, left_bottom, from_left, from_right, *outs):
-    half = right_top.shape[0]
+def merge_kernel(right_top, left_bottom, from_left, from_right, *outs):
     count, start = len(outs) // 2, 0
     for c in range(count):
         cols = slice(start, start + outs[c].shape[1])
         start = cols.stop
-        to_right, to_left = outs[c], outs[count + c]
-        to_right[:half, :] = (right_top[:, cols].astype(F32) + from_left[:, cols].astype(F32)).astype(BF16)
-        to_right[half:, :] = right_bottom[:, cols]
-        to_left[:half, :] = left_top[:, cols]
-        to_left[half:, :] = (left_bottom[:, cols].astype(F32) + from_right[:, cols].astype(F32)).astype(BF16)
-
-
-def finish(first_column):
-    def kernel(weights, tokens, top, bottom, from_left, from_right, arrived, straight, crossed, same_row, out):
-        half = top.shape[0]
+        outs[c][...] = (right_top[:, cols].astype(F32) + from_left[:, cols].astype(F32)).astype(BF16)
+        outs[count + c][...] = (left_bottom[:, cols].astype(F32) + from_right[:, cols].astype(F32)).astype(BF16)
+
+
+def finish(first_column, first_arrived):
+    def kernel(weights, tokens, *refs):
+        *parts, arrived, straight, crossed, same_row, out = refs
+        half = out.shape[0] // 2
         section, row, low = place_in_grid()
         factor = coefficients(weights, section)
         cols = slice(first_column, first_column + out.shape[1])
+        there = slice(first_arrived, first_arrived + out.shape[1])
         far, far_odd = kept(row == 3, factor(6)), kept(row == 3, jnp.where(low, factor(5), factor(7)))
         near = kept(jnp.logical_not(low), factor(1))
-        for own, base in ((top, 0), (bottom, half)):
+        for base, (own, plain, merged) in ((0, parts[:3]), (half, parts[3:])):
             for start in range(0, half, 16):
                 rows, here = slice(base + start, base + start + 16), slice(start, start + 16)
-                attention_sum = (
-                    own[here, cols].astype(F32) + from_left[rows, :].astype(F32) + from_right[rows, :].astype(F32)
-                )
+                attention_sum = own[here, cols].astype(F32) + plain[here, cols].astype(F32)
+                attention_sum = attention_sum + merged[here, :].astype(F32)
                 block_out = (tokens[rows, cols].astype(F32) + attention_sum).astype(BF16)
-                past = arrived[rows, :].astype(F32) + far * straight[rows, cols].astype(F32)
+                past = arrived[rows, there].astype(F32) + far * straight[rows, cols].astype(F32)
                 past = past + far_odd * crossed[rows, cols].astype(F32)
                 past = past + near * same_row[rows, cols].astype(F32)
                 out[rows, :] = (factor(0) * block_out.astype(F32) + past).astype(BF16)
 
     return kernel
+
+
+def cut(width, proportions):
+    return [width * part // sum(proportions) for part in proportions]
 
 
 def on_device(
@@ -275,7 +277,7 @@
 ):
     token_rows = section_input[0]
     rows, width = token_rows.shape
-    half, sizes = rows // 2, (int(width * SPLIT), width - int(width * SPLIT))
+    half, sizes = rows // 2, cut(width, CARRIED_PIECES)
     wq, wk, wv, wo = query_weight[0], key_weight[0], value_weight[0], output_weight[0]
     q_width = wq.shape[1]
     table = mix_weights.T
@@ -331,20 +333,24 @@
     left_out_top, left_out_bottom, right_out_top, right_out_bottom = on_chip(
         sides_kernel, [half_block] * 4, q1, kv0, kv1, kv3, wo
     )
+    plain_left, plain_right = around(right_out_bottom, 1), around(left_out_top, -1)
     own_top, own_bottom = on_chip(own_kernel, [half_block] * 2, q0, kv0, kv1, kv3, wo)
+    merged_sizes, pieces, first = cut(width, MERGED_PIECES), [], 0
     merged = on_chip(
-        merge_kernel, [((rows, size), BF16) for size in 2 * sizes],
-        right_out_top, right_out_bottom, left_out_top, left_out_bottom, from_left_merge, from_right_merge, limit=8,
-    )
-    pieces = []
-    for c, size in enumerate(sizes):
-        from_left = around(merged[c], 1)
-        from_right = around(merged[len(sizes) + c], -1)
+        merge_kernel, [((half, size), BF16) for size in 2 * merged_sizes],
+        right_out_top, left_out_bottom, from_left_merge, from_right_merge, limit=8,
+    )
+    for c, size in enumerate(merged_sizes):
+        merged_left = around(merged[c], 1)
+        merged_right = around(merged[len(merged_sizes) + c], -1)
+        piece = 0 if first + size <= sizes[0] else 1
         (mixed,) = on_chip(
-            finish(sum(sizes[:c])), [((rows, size), BF16)], table, token_rows, own_top, own_bottom,
-            from_left, from_right, arrived[c], far_even, far_odd, near_row, limit=8,
+            finish(first, first - sizes[0] * piece), [((rows, size), BF16)], table, token_rows,
+            own_top, plain_right, merged_left, own_bottom, plain_left, merged_right,
+            arrived[piece], far_even, far_odd, near_row, limit=8,
         )
         pieces.append(to_next_section(mixed))
+        first += size
     return jnp.concatenate(pieces, axis=1)[None]
 
 

time: 114 us -> 118 us (1.035)
  starting transfers between devices: 42.7 us -> 56.5 us
  waiting for transfers between devices: 46.1 us -> 36.6 us
    ppermute x9, waiting for transfers between devices: 16.9 us -> 3.69 us  [sent(): return lax.ppermute(value, 'section', [(i, i + steps(i)) for i in sources])]
    ppermute x10 -> x14, starting transfers between devices: 15.9 us -> 22.7 us  [around(): lax.ppermute(value, 'tensor', [(i, (i + steps) % count) for i in range(co...]
    ppermute x9, starting transfers between devices: 26.6 us -> 32.5 us  [sent(): return lax.ppermute(value, 'section', [(i, i + steps(i)) for i in sources])]
    ppermute x10 -> x14, waiting for transfers between devices: 14.6 us -> 17.7 us  [around(): lax.ppermute(value, 'tensor', [(i, (i + steps) % count) for i in range(co...]
    ppermute x2 -> x3, starting transfers between devices: 0.15 us -> 1.35 us  [to_next_section(): lax.ppermute(block, 'section', [(i, (i + 1) % count) for i in range(count)])]
    ppermute x2 -> x3, waiting for transfers between devices: 14.6 us -> 15.2 us  [to_next_section(): lax.ppermute(block, 'section', [(i, (i + 1) % count) for i in range(count)])]
    pallas_call x14 -> x15, Pallas kernels: 23.1 us -> 23.1 us  [on_chip(): pl.pallas_call(body, out_shape=[pltpu.VMEM(shape, dtype) for shape, dtype...]
  transfers between devices with their start and end apart: 21 -> 26, of which waited for: 9 -> 9; matrix products, arithmetic and copies ran while one was open for 0% -> 0% of each run, Pallas kernels for 19% -> 18%
where the time goes in v2:
time: 118 us
  starting transfers between devices  56.5 us (48%)
  waiting for transfers between devices  36.6 us (31%)
  Pallas kernels  23.1 us (20%)
    ppermute x9, starting transfers between devices, sent(): return lax.ppermute(value, 'section', [(i, i + steps(i)) for i in sources])  32.5 us
    pallas_call x15, Pallas kernels, on_chip(): pl.pallas_call(body, out_shape=[pltpu.VMEM(shape, dtype) for shape, dtype...  23.1 us
    ppermute x14, starting transfers between devices, around(): lax.ppermute(value, 'tensor', [(i, (i + steps) % count) for i in range(co...  22.7 us
    ppermute x14, waiting for transfers between devices, around(): lax.ppermute(value, 'tensor', [(i, (i + steps) % count) for i in range(co...  17.7 us
    ppermute x3, waiting for transfers between devices, to_next_section(): lax.ppermute(block, 'section', [(i, (i + 1) % count) for i in range(count)])  15.2 us
    ppermute x9, waiting for transfers between devices, sent(): return lax.ppermute(value, 'section', [(i, i + steps(i)) for i in sources])  3.69 us
  transfers between devices with their start and end apart: 26, of which 9 were waited for; matrix products, arithmetic and copies ran while one was open for 0% of the time, Pallas kernels for 18%

profile of v2, /device:TPU:0, one launch (start us, length us, event | category | flops | bytes accessed | tf_op | source)
XLA Modules:
  0.0 117.8 jit_solution(8394621799832860627)
XLA Ops:
  0.0 1.9 %shard_map.73 = (bf16[128,4096]{1,0:T(8,128)(2,1)S(1)}, bf16[128,4096]{1,0:T(8,128)(2,1)S(1)}, bf16[128,4096]{1,0:T(8,128)(2,1)S(1)}) custom-call(bf16[128,4096]{1,0:T(8,128)(2,1)} %bitcast.19, bf16[7,128,4096]{2,1,0:T(8,128)(2,1)} %bitcast.29), custom_call_target="tpu_custom_call" | custom-call | tf_op jit(solution)/shard_map/pallas_call | solution.py:42
  1.9 2.9 %collective-permute-start.1 = (bf16[128,4096]{1,0:T(8,128)(2,1)S(1)}, bf16[128,4096]{1,0:T(8,128)(2,1)S(1)}, u32[]{:S(2)}, u32[]{:S(2)}) collective-permute-start(bf16[128,4096]{1,0:T(8,128)(2,1)S(1)} %get-tuple-element.34.refs_0_), channel_id=1, source_target_pairs={{0,3},{1,0},{2,1},{3,2},{4,7},{5,4},{6,5},{7,6},{8,11},{9,8},{10,9... | collective-permute-start | bytes 3145736 | tf_op jit(solution)/shard_map/ppermute | solution.py:24
  4.8 5.8 %collective-permute-start.10 = (bf16[128,4096]{1,0:T(8,128)(2,1)S(1)}, bf16[128,4096]{1,0:T(8,128)(2,1)S(1)}, u32[]{:S(2)}, u32[]{:S(2)}) collective-permute-start(bf16[128,4096]{1,0:T(8,128)(2,1)S(1)} %get-tuple-element.51), channel_id=1, source_target_pairs={{0,16},{4,20},{8,24},{12,28},{16,0},{20,4},{24,8},{28,12},{32,48},... | collective-permute-start | bytes 3145736 | tf_op jit(solution)/shard_map/ppermute | solution.py:28
  10.6 3.2 %collective-permute-start.15 = (bf16[128,4096]{1,0:T(8,128)(2,1)S(1)}, bf16[128,4096]{1,0:T(8,128)(2,1)S(1)}, u32[]{:S(2)}, u32[]{:S(2)}) collective-permute-start(bf16[128,4096]{1,0:T(8,128)(2,1)S(1)} %get-tuple-element.56), channel_id=1, source_target_pairs={{0,112},{4,116},{8,120},{12,124},{16,96},{20,100},{24,104},{28,108... | collective-permute-start | bytes 3145736 | tf_op jit(solution)/shard_map/ppermute | solution.py:28
  13.9 2.7 %shard_map.81 = (bf16[128,4096]{1,0:T(8,128)(2,1)S(1)}, bf16[128,4096]{1,0:T(8,128)(2,1)S(1)}, bf16[128,4096]{1,0:T(8,128)(2,1)S(1)}, bf16[128,4096]{1,0:T(8,128)(2,1)S(1)}, bf16[128,4096]{1,0:T(8,128)(2,1)S(1)}) custom-call(bf16[7,128,4096]{2,1,0:T(8,128)(2,1)} %bitcast.30), custom_call_target="tpu_custom_call" | custom-call | tf_op jit(solution)/shard_map/pallas_call | solution.py:42
  16.6 2.1 %collective-permute-start.11 = (bf16[128,4096]{1,0:T(8,128)(2,1)S(1)}, bf16[128,4096]{1,0:T(8,128)(2,1)S(1)}, u32[]{:S(2)}, u32[]{:S(2)}) collective-permute-start(bf16[128,4096]{1,0:T(8,128)(2,1)S(1)} %get-tuple-element.52), channel_id=1, source_target_pairs={{0,16},{4,20},{8,24},{12,28},{16,0},{20,4},{24,8},{28,12},{32,48},... | collective-permute-start | bytes 3145736 | tf_op jit(solution)/shard_map/ppermute | solution.py:28
  18.7 8.6 %collective-permute-done.1.refs_1_ = bf16[128,4096]{1,0:T(8,128)(2,1)S(1)} collective-permute-done((bf16[128,4096]{1,0:T(8,128)(2,1)S(1)}, bf16[128,4096]{1,0:T(8,128)(2,1)S(1)}, u32[]{:S(2)}, u32[]{:S(2)}) %collective-permute-start.1) | collective-permute-done | bytes 1048608 | tf_op jit(solution)/shard_map/ppermute | solution.py:24
  27.3 3.8 %collective-permute-start.3 = (bf16[64,4096]{1,0:T(8,128)(2,1)S(1)}, bf16[64,4096]{1,0:T(8,128)(2,1)S(1)}, u32[]{:S(2)}, u32[]{:S(2)}) collective-permute-start(bf16[64,4096]{1,0:T(8,128)(2,1)S(1)} %slice.9), channel_id=1, source_target_pairs={{0,3},{1,0},{2,1},{3,2},{4,7},{5,4},{6,5},{7,6},{8,11},{9,8},{10,9... | collective-permute-start | bytes 1572872 | tf_op jit(solution)/shard_map/ppermute | solution.py:24
  31.1 0.1 collective-permute-start.2
  31.2 3.4 %collective-permute-done.10.crossed.crossed_early = bf16[128,4096]{1,0:T(8,128)(2,1)S(1)} collective-permute-done((bf16[128,4096]{1,0:T(8,128)(2,1)S(1)}, bf16[128,4096]{1,0:T(8,128)(2,1)S(1)}, u32[]{:S(2)}, u32[]{:S(2)}) %collective-permute-start.10) | collective-permute-done | bytes 1048608 | tf_op jit(solution)/shard_map/ppermute | solution.py:28
  34.6 1.6 %collective-permute-start.14 = (bf16[128,4096]{1,0:T(8,128)(2,1)S(1)}, bf16[128,4096]{1,0:T(8,128)(2,1)S(1)}, u32[]{:S(2)}, u32[]{:S(2)}) collective-permute-start(bf16[128,4096]{1,0:T(8,128)(2,1)S(1)} %get-tuple-element.55), channel_id=1, source_target_pairs={{0,96},{4,100},{8,104},{12,108},{16,112},{20,116},{24,120},{28,124... | collective-permute-start | bytes 3145736 | tf_op jit(solution)/shard_map/ppermute | solution.py:28
  36.2 0.5 shard_map.82
  36.7 0.2 collective-permute-done.15.refs_8_
  36.9 2.4 %collective-permute-start.23 = (bf16[128,1536]{1,0:T(8,128)(2,1)S(1)}, bf16[128,1536]{1,0:T(8,128)(2,1)S(1)}, u32[]{:S(2)}, u32[]{:S(2)}) collective-permute-start(bf16[128,1536]{1,0:T(8,128)(2,1)S(1)} %get-tuple-element.62), channel_id=1, source_target_pairs={{0,32},{4,36},{8,40},{12,44},{16,48},{20,52},{24,56},{28,60},{32,6... | collective-permute-start | bytes 1179656 | tf_op jit(solution)/shard_map/ppermute | solution.py:28
  39.4 2.0 %collective-permute-done.3.bottom = bf16[64,4096]{1,0:T(8,128)(2,1)S(1)} collective-permute-done((bf16[64,4096]{1,0:T(8,128)(2,1)S(1)}, bf16[64,4096]{1,0:T(8,128)(2,1)S(1)}, u32[]{:S(2)}, u32[]{:S(2)}) %collective-permute-start.3) | collective-permute-done | bytes 524320 | tf_op jit(solution)/shard_map/ppermute | solution.py:24
  41.4 5.8 %collective-permute-start.16 = (bf16[128,4096]{1,0:T(8,128)(2,1)S(1)}, bf16[128,4096]{1,0:T(8,128)(2,1)S(1)}, u32[]{:S(2)}, u32[]{:S(2)}) collective-permute-start(bf16[128,4096]{1,0:T(8,128)(2,1)S(1)} %get-tuple-element.57), channel_id=1, source_target_pairs={{0,16},{4,20},{8,24},{12,28},{32,48},{36,52},{40,56},{44,60},{64,8... | collective-permute-start | bytes 3145736 | tf_op jit(solution)/shard_map/ppermute | solution.py:28
  47.2 3.5 %collective-permute-start.12 = (bf16[128,2560]{1,0:T(8,128)(2,1)S(1)}, bf16[128,2560]{1,0:T(8,128)(2,1)S(1)}, u32[]{:S(2)}, u32[]{:S(2)}) collective-permute-start(bf16[128,2560]{1,0:T(8,128)(2,1)S(1)} %get-tuple-element.54), channel_id=1, source_target_pairs={{0,32},{4,36},{8,40},{12,44},{16,48},{20,52},{24,56},{28,60},{32,6... | collective-permute-start | bytes 1966088 | tf_op jit(solution)/shard_map/ppermute | solution.py:28
  50.8 1.6 %shard_map.74.refs_2_.refs_3_.joined = bf16[4096,256]{1,0:T(8,128)(2,1)S(1)} custom-call(bf16[4096,128]{1,0:T(8,128)(2,1)} %bitcast.31, bf16[4096,128]{1,0:T(8,128)(2,1)} %bitcast.32), custom_call_target="tpu_custom_call" | custom-call | tf_op jit(solution)/shard_map/pallas_call | solution.py:42
  52.4 1.3 %shard_map.75 = (bf16[128,768]{1,0:T(8,128)(2,1)S(1)}, bf16[128,1024]{1,0:T(8,128)(2,1)S(1)}) custom-call(bf16[128,4096]{1,0:T(8,128)(2,1)S(1)} %get-tuple-element.34.refs_0_, bf16[4096,768]{1,0:T(8,128)(2,1)S(1)} %bitcast.11, bf16[4096,256]{1,0:T(8,128)(2,1)S(1)} %shard_map.74.refs_2_.refs_3_.joined), custom_call_target="tpu_custom_call" | custom-call | tf_op jit(solution)/shard_map/pallas_call | solution.py:42
  53.7 2.4 %shard_map.76 = (bf16[256,768]{1,0:T(8,128)(2,1)S(1)}, bf16[256,1024]{1,0:T(8,128)(2,1)S(1)}) custom-call(bf16[128,4096]{1,0:T(8,128)(2,1)S(1)} %collective-permute-done.refs_0_, bf16[128,4096]{1,0:T(8,128)(2,1)S(1)} %collective-permute-done.1.refs_1_, bf16[4096,768]{1,0:T(8,128)(2,1)S(1)} %bitcast.12, bf16[4096,256]{1,0:T(8,128)(2,1)S(1)} %shard_map.74.refs_2_.refs_3_.joined), custom_call_target="tpu_custom_call" | custom-call | tf_op jit(solution)/shard_map/pallas_call | solution.py:42
  56.1 3.4 %shard_map.77 = (bf16[64,4096]{1,0:T(8,128)(2,1)S(1)}, bf16[64,4096]{1,0:T(8,128)(2,1)S(1)}, bf16[128,1024]{1,0:T(8,128)(2,1)S(1)}) custom-call(bf16[64,4096]{1,0:T(8,128)(2,1)S(1)} %collective-permute-done.2.top, bf16[64,4096]{1,0:T(8,128)(2,1)S(1)} %collective-permute-done.3.bottom, bf16[4096,768]{1,0:T(8,128)(2,1)S(1)} %bitcast.13, ...), custom_call_target="tpu_custom_call" | custom-call | tf_op jit(solution)/shard_map/pallas_call | solution.py:42
  59.6 0.1 collective-permute-start.5
  59.7 3.8 %collective-permute-start.6 = (bf16[64,4096]{1,0:T(8,128)(2,1)S(1)}, bf16[64,4096]{1,0:T(8,128)(2,1)S(1)}, u32[]{:S(2)}, u32[]{:S(2)}) collective-permute-start(bf16[64,4096]{1,0:T(8,128)(2,1)S(1)} %get-tuple-element.45), channel_id=1, source_target_pairs={{0,3},{1,0},{2,1},{3,2},{4,7},{5,4},{6,5},{7,6},{8,11},{9,8},{10,9... | collective-permute-start | bytes 1572872 | tf_op jit(solution)/shard_map/ppermute | solution.py:24
  63.4 0.4 shard_map.86
  63.8 3.6 %collective-permute-start.24 = (bf16[128,1536]{1,0:T(8,128)(2,1)S(1)}, bf16[128,1536]{1,0:T(8,128)(2,1)S(1)}, u32[]{:S(2)}, u32[]{:S(2)}) collective-permute-start(bf16[128,1536]{1,0:T(8,128)(2,1)S(1)} %shard_map.86), channel_id=1, source_target_pairs={{0,32},{4,36},{8,40},{12,44},{16,48},{20,52},{24,56},{28,60},{32,6... | collective-permute-start | bytes 1179656 | tf_op jit(solution)/shard_map/ppermute | solution.py:28
  67.5 4.2 %shard_map.79 = (bf16[64,4096]{1,0:T(8,128)(2,1)S(1)}, bf16[64,4096]{1,0:T(8,128)(2,1)S(1)}, bf16[64,4096]{1,0:T(8,128)(2,1)S(1)}, bf16[64,4096]{1,0:T(8,128)(2,1)S(1)}) custom-call(bf16[256,768]{1,0:T(8,128)(2,1)S(1)} %get-tuple-element.40.query, bf16[128,1024]{1,0:T(8,128)(2,1)S(1)} %get-tuple-element.36.kv0, bf16[256,1024]{1,0:T(8,128)(2,1)S(1)} %get-tuple-element.37.kv1, ...), custom_call_target="tpu_custom_call" | custom-call | tf_op jit(solution)/shard_map/pallas_call | solution.py:42
  71.7 2.0 %collective-permute-start.4 = (bf16[64,4096]{1,0:T(8,128)(2,1)S(1)}, bf16[64,4096]{1,0:T(8,128)(2,1)S(1)}, u32[]{:S(2)}, u32[]{:S(2)}) collective-permute-start(bf16[64,4096]{1,0:T(8,128)(2,1)S(1)} %get-tuple-element.41), channel_id=1, source_target_pairs={{0,3},{1,0},{2,1},{3,2},{4,7},{5,4},{6,5},{7,6},{8,11},{9,8},{10,9... | collective-permute-start | bytes 1572872 | tf_op jit(solution)/shard_map/ppermute | solution.py:24
  73.7 0.1 collective-permute-start.8
  73.8 0.6 shard_map.83
  74.4 4.4 %collective-permute-start.13 = (bf16[128,2560]{1,0:T(8,128)(2,1)S(1)}, bf16[128,2560]{1,0:T(8,128)(2,1)S(1)}, u32[]{:S(2)}, u32[]{:S(2)}) collective-permute-start(bf16[128,2560]{1,0:T(8,128)(2,1)S(1)} %shard_map.83), channel_id=1, source_target_pairs={{0,32},{4,36},{8,40},{12,44},{16,48},{20,52},{24,56},{28,60},{32,6... | collective-permute-start | bytes 1966088 | tf_op jit(solution)/shard_map/ppermute | solution.py:28
  78.9 0.2 shard_map.80
  79.1 2.2 %collective-permute-start.21 = (bf16[64,1536]{1,0:T(8,128)(2,1)S(1)}, bf16[64,1536]{1,0:T(8,128)(2,1)S(1)}, u32[]{:S(2)}, u32[]{:S(2)}) collective-permute-start(bf16[64,1536]{1,0:T(8,128)(2,1)S(1)} %get-tuple-element.60), channel_id=1, source_target_pairs={{0,1},{1,2},{2,3},{3,0},{4,5},{5,6},{6,7},{7,4},{8,9},{9,10},{10,1... | collective-permute-start | bytes 589832 | tf_op jit(solution)/shard_map/ppermute | solution.py:24
  81.4 1.6 %collective-permute-start.22 = (bf16[64,1536]{1,0:T(8,128)(2,1)S(1)}, bf16[64,1536]{1,0:T(8,128)(2,1)S(1)}, u32[]{:S(2)}, u32[]{:S(2)}) collective-permute-start(bf16[64,1536]{1,0:T(8,128)(2,1)S(1)} %get-tuple-element.61), channel_id=1, source_target_pairs={{0,3},{1,0},{2,1},{3,2},{4,7},{5,4},{6,5},{7,6},{8,11},{9,8},{10,9... | collective-permute-start | bytes 589832 | tf_op jit(solution)/shard_map/ppermute | solution.py:24
  83.0 3.1 %collective-permute-done.4.refs_1_ = bf16[64,4096]{1,0:T(8,128)(2,1)S(1)} collective-permute-done((bf16[64,4096]{1,0:T(8,128)(2,1)S(1)}, bf16[64,4096]{1,0:T(8,128)(2,1)S(1)}, u32[]{:S(2)}, u32[]{:S(2)}) %collective-permute-start.4) | collective-permute-done | bytes 524320 | tf_op jit(solution)/shard_map/ppermute | solution.py:24
  86.1 2.0 %collective-permute-start.7 = (bf16[64,1280]{1,0:T(8,128)(2,1)S(1)}, bf16[64,1280]{1,0:T(8,128)(2,1)S(1)}, u32[]{:S(2)}, u32[]{:S(2)}) collective-permute-start(bf16[64,1280]{1,0:T(8,128)(2,1)S(1)} %get-tuple-element.46), channel_id=1, source_target_pairs={{0,1},{1,2},{2,3},{3,0},{4,5},{5,6},{6,7},{7,4},{8,9},{9,10},{10,1... | collective-permute-start | bytes 491528 | tf_op jit(solution)/shard_map/ppermute | solution.py:24
  88.1 0.8 collective-permute-done.8.refs_4_
  88.9 0.9 collective-permute-start.9
  89.8 3.2 %collective-permute-done.21.refs_2_ = bf16[64,1536]{1,0:T(8,128)(2,1)S(1)} collective-permute-done((bf16[64,1536]{1,0:T(8,128)(2,1)S(1)}, bf16[64,1536]{1,0:T(8,128)(2,1)S(1)}, u32[]{:S(2)}, u32[]{:S(2)}) %collective-permute-start.21) | collective-permute-done | bytes 196640 | tf_op jit(solution)/shard_map/ppermute | solution.py:24
  93.0 3.2 %collective-permute-start.19 = (bf16[64,1280]{1,0:T(8,128)(2,1)S(1)}, bf16[64,1280]{1,0:T(8,128)(2,1)S(1)}, u32[]{:S(2)}, u32[]{:S(2)}) collective-permute-start(bf16[64,1280]{1,0:T(8,128)(2,1)S(1)} %get-tuple-element.59), channel_id=1, source_target_pairs={{0,3},{1,0},{2,1},{3,2},{4,7},{5,4},{6,5},{7,6},{8,11},{9,8},{10,9... | collective-permute-start | bytes 491528 | tf_op jit(solution)/shard_map/ppermute | solution.py:24
  96.2 2.2 %shard_map.78 = (bf16[64,4096]{1,0:T(8,128)(2,1)S(1)}, bf16[64,4096]{1,0:T(8,128)(2,1)S(1)}) custom-call(bf16[128,768]{1,0:T(8,128)(2,1)S(1)} %get-tuple-element.35.query, bf16[128,1024]{1,0:T(8,128)(2,1)S(1)} %get-tuple-element.36.kv0, bf16[256,1024]{1,0:T(8,128)(2,1)S(1)} %get-tuple-element.37.kv1, bf16[128,1024]{1,0:T(8,128)(2,1)S(1)} %get-tuple-element.38.kv3, ...), custom_call_target="tpu_custom_call" | custom-call | tf_op jit(solution)/shard_map/pallas_call | solution.py:42
  98.5 0.6 shard_map.87
  99.2 0.5 shard_map.84
  99.7 1.2 collective-permute-start.17
  100.9 0.5 shard_map.85
  101.4 0.1 collective-permute-start.20
  101.5 11.7 %collective-permute-done.17 = bf16[128,1280]{1,0:T(8,128)(2,1)S(1)} collective-permute-done((bf16[128,1280]{1,0:T(8,128)(2,1)S(1)}, bf16[128,1280]{1,0:T(8,128)(2,1)S(1)}, u32[]{:S(2)}, u32[]{:S(2)}) %collective-permute-start.17) | collective-permute-done | bytes 327712 | tf_op jit(solution)/shard_map/ppermute | solution.py:33
  113.2 3.5 %collective-permute-done.20 = bf16[128,1280]{1,0:T(8,128)(2,1)S(1)} collective-permute-done((bf16[128,1280]{1,0:T(8,128)(2,1)S(1)}, bf16[128,1280]{1,0:T(8,128)(2,1)S(1)}, u32[]{:S(2)}, u32[]{:S(2)}) %collective-permute-start.20) | collective-permute-done | bytes 327712 | tf_op jit(solution)/shard_map/ppermute | solution.py:33
  116.7 1.1 maximum_bitcast_fusion
  (36 shorter events, 0.2 us)
Async XLA Ops:
  1.9 25.4 %collective-permute-start.1 = (bf16[128,4096]{1,0:T(8,128)(2,1)S(1)}, bf16[128,4096]{1,0:T(8,128)(2,1)S(1)}, u32[]{:S(2)}, u32[]{:S(2)}) collective-permute-start(bf16[128,4096]{1,0:T(8,128)(2,1)S(1)} %get-tuple-element.34.refs_0_), channel_id=1, source_target_pairs={{0,3},{1,0},{2,1},{3,2},{4,7},{5,4},{6,5},{7,6},{8,11},{9,8},{10,9... | collective-permute-start | bytes 3145736 | tf_op jit(solution)/shard_map/ppermute | solution.py:24
  4.8 26.2 %collective-permute-start = (bf16[128,4096]{1,0:T(8,128)(2,1)S(1)}, bf16[128,4096]{1,0:T(8,128)(2,1)S(1)}, u32[]{:S(2)}, u32[]{:S(2)}) collective-permute-start(bf16[128,4096]{1,0:T(8,128)(2,1)S(1)} %get-tuple-element.34.refs_0_), channel_id=1, source_target_pairs={{0,1},{1,2},{2,3},{3,0},{4,5},{5,6},{6,7},{7,4},{8,9},{9,10},{10,1... | collective-permute-start | bytes 3145736 | tf_op jit(solution)/shard_map/ppermute | solution.py:24
  4.8 29.8 %collective-permute-start.10 = (bf16[128,4096]{1,0:T(8,128)(2,1)S(1)}, bf16[128,4096]{1,0:T(8,128)(2,1)S(1)}, u32[]{:S(2)}, u32[]{:S(2)}) collective-permute-start(bf16[128,4096]{1,0:T(8,128)(2,1)S(1)} %get-tuple-element.51), channel_id=1, source_target_pairs={{0,16},{4,20},{8,24},{12,28},{16,0},{20,4},{24,8},{28,12},{32,48},... | collective-permute-start | bytes 3145736 | tf_op jit(solution)/shard_map/ppermute | solution.py:28
  10.6 26.3 %collective-permute-start.15 = (bf16[128,4096]{1,0:T(8,128)(2,1)S(1)}, bf16[128,4096]{1,0:T(8,128)(2,1)S(1)}, u32[]{:S(2)}, u32[]{:S(2)}) collective-permute-start(bf16[128,4096]{1,0:T(8,128)(2,1)S(1)} %get-tuple-element.56), channel_id=1, source_target_pairs={{0,112},{4,116},{8,120},{12,124},{16,96},{20,100},{24,104},{28,108... | collective-permute-start | bytes 3145736 | tf_op jit(solution)/shard_map/ppermute | solution.py:28
  13.9 38.5 %slice-start = ((s8[6291456]{0:T(1024)(128)(4,1)}), s8[4194304]{0:T(1024)(128)(4,1)S(1)}, s32[]{:S(2)}) async-start(s8[6291456]{0:T(1024)(128)(4,1)} %bitcast.9), calls=%async_computation | async-start | bytes 8388608
  16.6 19.6 %copy-start.1 = (f32[32,8]{0,1:T(8,128)S(1)}, f32[32,8]{0,1:T(8,128)}, u32[]{:S(2)}) copy-start(f32[32,8]{0,1:T(8,128)} %param.13) | copy-start | bytes 3076
  16.6 35.7 %slice-start.1 = ((s8[6291456]{0:T(1024)(128)(4,1)}), s8[2097152]{0:T(1024)(128)(4,1)S(1)}, s32[]{:S(2)}) async-start(s8[6291456]{0:T(1024)(128)(4,1)} %bitcast.9), calls=%async_computation.1 | async-start | bytes 4194304
  16.6 43.0 %collective-permute-start.11 = (bf16[128,4096]{1,0:T(8,128)(2,1)S(1)}, bf16[128,4096]{1,0:T(8,128)(2,1)S(1)}, u32[]{:S(2)}, u32[]{:S(2)}) collective-permute-start(bf16[128,4096]{1,0:T(8,128)(2,1)S(1)} %get-tuple-element.52), channel_id=1, source_target_pairs={{0,16},{4,20},{8,24},{12,28},{16,0},{20,4},{24,8},{28,12},{32,48},... | collective-permute-start | bytes 3145736 | tf_op jit(solution)/shard_map/ppermute | solution.py:28
  27.3 14.1 %collective-permute-start.3 = (bf16[64,4096]{1,0:T(8,128)(2,1)S(1)}, bf16[64,4096]{1,0:T(8,128)(2,1)S(1)}, u32[]{:S(2)}, u32[]{:S(2)}) collective-permute-start(bf16[64,4096]{1,0:T(8,128)(2,1)S(1)} %slice.9), channel_id=1, source_target_pairs={{0,3},{1,0},{2,1},{3,2},{4,7},{5,4},{6,5},{7,6},{8,11},{9,8},{10,9... | collective-permute-start | bytes 1572872 | tf_op jit(solution)/shard_map/ppermute | solution.py:24
  31.1 16.1 %collective-permute-start.2 = (bf16[64,4096]{1,0:T(8,128)(2,1)S(1)}, bf16[64,4096]{1,0:T(8,128)(2,1)S(1)}, u32[]{:S(2)}, u32[]{:S(2)}) collective-permute-start(bf16[64,4096]{1,0:T(8,128)(2,1)S(1)} %slice.8), channel_id=1, source_target_pairs={{0,1},{1,2},{2,3},{3,0},{4,5},{5,6},{6,7},{7,4},{8,9},{9,10},{10,1... | collective-permute-start | bytes 1572872 | tf_op jit(solution)/shard_map/ppermute | solution.py:24
  34.6 29.2 %collective-permute-start.14 = (bf16[128,4096]{1,0:T(8,128)(2,1)S(1)}, bf16[128,4096]{1,0:T(8,128)(2,1)S(1)}, u32[]{:S(2)}, u32[]{:S(2)}) collective-permute-start(bf16[128,4096]{1,0:T(8,128)(2,1)S(1)} %get-tuple-element.55), channel_id=1, source_target_pairs={{0,96},{4,100},{8,104},{12,108},{16,112},{20,116},{24,120},{28,124... | collective-permute-start | bytes 3145736 | tf_op jit(solution)/shard_map/ppermute | solution.py:28
  36.9 22.7 %collective-permute-start.23 = (bf16[128,1536]{1,0:T(8,128)(2,1)S(1)}, bf16[128,1536]{1,0:T(8,128)(2,1)S(1)}, u32[]{:S(2)}, u32[]{:S(2)}) collective-permute-start(bf16[128,1536]{1,0:T(8,128)(2,1)S(1)} %get-tuple-element.62), channel_id=1, source_target_pairs={{0,32},{4,36},{8,40},{12,44},{16,48},{20,52},{24,56},{28,60},{32,6... | collective-permute-start | bytes 1179656 | tf_op jit(solution)/shard_map/ppermute | solution.py:28
  41.4 37.7 %collective-permute-start.16 = (bf16[128,4096]{1,0:T(8,128)(2,1)S(1)}, bf16[128,4096]{1,0:T(8,128)(2,1)S(1)}, u32[]{:S(2)}, u32[]{:S(2)}) collective-permute-start(bf16[128,4096]{1,0:T(8,128)(2,1)S(1)} %get-tuple-element.57), channel_id=1, source_target_pairs={{0,16},{4,20},{8,24},{12,28},{32,48},{36,52},{40,56},{44,60},{64,8... | collective-permute-start | bytes 3145736 | tf_op jit(solution)/shard_map/ppermute | solution.py:28
  47.2 24.5 %collective-permute-start.12 = (bf16[128,2560]{1,0:T(8,128)(2,1)S(1)}, bf16[128,2560]{1,0:T(8,128)(2,1)S(1)}, u32[]{:S(2)}, u32[]{:S(2)}) collective-permute-start(bf16[128,2560]{1,0:T(8,128)(2,1)S(1)} %get-tuple-element.54), channel_id=1, source_target_pairs={{0,32},{4,36},{8,40},{12,44},{16,48},{20,52},{24,56},{28,60},{32,6... | collective-permute-start | bytes 1966088 | tf_op jit(solution)/shard_map/ppermute | solution.py:28
  52.4 3.8 %slice-start.2 = ((s8[6291456]{0:T(1024)(128)(4,1)}), s8[4194304]{0:T(1024)(128)(4,1)S(1)}, s32[]{:S(2)}) async-start(s8[6291456]{0:T(1024)(128)(4,1)} %bitcast.14), calls=%async_computation.2 | async-start | bytes 8388608
  53.7 2.4 %slice-start.3 = ((s8[6291456]{0:T(1024)(128)(4,1)}), s8[2097152]{0:T(1024)(128)(4,1)S(1)}, s32[]{:S(2)}) async-start(s8[6291456]{0:T(1024)(128)(4,1)} %bitcast.14), calls=%async_computation.3 | async-start | bytes 4194304
  59.6 14.2 %collective-permute-start.5 = (bf16[64,4096]{1,0:T(8,128)(2,1)S(1)}, bf16[64,4096]{1,0:T(8,128)(2,1)S(1)}, u32[]{:S(2)}, u32[]{:S(2)}) collective-permute-start(bf16[64,4096]{1,0:T(8,128)(2,1)S(1)} %get-tuple-element.44), channel_id=1, source_target_pairs={{0,1},{1,2},{2,3},{3,0},{4,5},{5,6},{6,7},{7,4},{8,9},{9,10},{10,1... | collective-permute-start | bytes 1572872 | tf_op jit(solution)/shard_map/ppermute | solution.py:24
  59.7 14.7 %collective-permute-start.6 = (bf16[64,4096]{1,0:T(8,128)(2,1)S(1)}, bf16[64,4096]{1,0:T(8,128)(2,1)S(1)}, u32[]{:S(2)}, u32[]{:S(2)}) collective-permute-start(bf16[64,4096]{1,0:T(8,128)(2,1)S(1)} %get-tuple-element.45), channel_id=1, source_target_pairs={{0,3},{1,0},{2,1},{3,2},{4,7},{5,4},{6,5},{7,6},{8,11},{9,8},{10,9... | collective-permute-start | bytes 1572872 | tf_op jit(solution)/shard_map/ppermute | solution.py:24
  63.8 17.5 %collective-permute-start.24 = (bf16[128,1536]{1,0:T(8,128)(2,1)S(1)}, bf16[128,1536]{1,0:T(8,128)(2,1)S(1)}, u32[]{:S(2)}, u32[]{:S(2)}) collective-permute-start(bf16[128,1536]{1,0:T(8,128)(2,1)S(1)} %shard_map.86), channel_id=1, source_target_pairs={{0,32},{4,36},{8,40},{12,44},{16,48},{20,52},{24,56},{28,60},{32,6... | collective-permute-start | bytes 1179656 | tf_op jit(solution)/shard_map/ppermute | solution.py:28
  71.7 14.3 %collective-permute-start.4 = (bf16[64,4096]{1,0:T(8,128)(2,1)S(1)}, bf16[64,4096]{1,0:T(8,128)(2,1)S(1)}, u32[]{:S(2)}, u32[]{:S(2)}) collective-permute-start(bf16[64,4096]{1,0:T(8,128)(2,1)S(1)} %get-tuple-element.41), channel_id=1, source_target_pairs={{0,3},{1,0},{2,1},{3,2},{4,7},{5,4},{6,5},{7,6},{8,11},{9,8},{10,9... | collective-permute-start | bytes 1572872 | tf_op jit(solution)/shard_map/ppermute | solution.py:24
  73.7 15.1 %collective-permute-start.8 = (bf16[64,4096]{1,0:T(8,128)(2,1)S(1)}, bf16[64,4096]{1,0:T(8,128)(2,1)S(1)}, u32[]{:S(2)}, u32[]{:S(2)}) collective-permute-start(bf16[64,4096]{1,0:T(8,128)(2,1)S(1)} %get-tuple-element.48), channel_id=1, source_target_pairs={{0,1},{1,2},{2,3},{3,0},{4,5},{5,6},{6,7},{7,4},{8,9},{9,10},{10,1... | collective-permute-start | bytes 1572872 | tf_op jit(solution)/shard_map/ppermute | solution.py:24
  74.4 24.7 %collective-permute-start.13 = (bf16[128,2560]{1,0:T(8,128)(2,1)S(1)}, bf16[128,2560]{1,0:T(8,128)(2,1)S(1)}, u32[]{:S(2)}, u32[]{:S(2)}) collective-permute-start(bf16[128,2560]{1,0:T(8,128)(2,1)S(1)} %shard_map.83), channel_id=1, source_target_pairs={{0,32},{4,36},{8,40},{12,44},{16,48},{20,52},{24,56},{28,60},{32,6... | collective-permute-start | bytes 1966088 | tf_op jit(solution)/shard_map/ppermute | solution.py:28
  79.1 13.8 %collective-permute-start.21 = (bf16[64,1536]{1,0:T(8,128)(2,1)S(1)}, bf16[64,1536]{1,0:T(8,128)(2,1)S(1)}, u32[]{:S(2)}, u32[]{:S(2)}) collective-permute-start(bf16[64,1536]{1,0:T(8,128)(2,1)S(1)} %get-tuple-element.60), channel_id=1, source_target_pairs={{0,1},{1,2},{2,3},{3,0},{4,5},{5,6},{6,7},{7,4},{8,9},{9,10},{10,1... | collective-permute-start | bytes 589832 | tf_op jit(solution)/shard_map/ppermute | solution.py:24
  81.4 11.6 %collective-permute-start.22 = (bf16[64,1536]{1,0:T(8,128)(2,1)S(1)}, bf16[64,1536]{1,0:T(8,128)(2,1)S(1)}, u32[]{:S(2)}, u32[]{:S(2)}) collective-permute-start(bf16[64,1536]{1,0:T(8,128)(2,1)S(1)} %get-tuple-element.61), channel_id=1, source_target_pairs={{0,3},{1,0},{2,1},{3,2},{4,7},{5,4},{6,5},{7,6},{8,11},{9,8},{10,9... | collective-permute-start | bytes 589832 | tf_op jit(solution)/shard_map/ppermute | solution.py:24
  86.1 13.0 %collective-permute-start.7 = (bf16[64,1280]{1,0:T(8,128)(2,1)S(1)}, bf16[64,1280]{1,0:T(8,128)(2,1)S(1)}, u32[]{:S(2)}, u32[]{:S(2)}) collective-permute-start(bf16[64,1280]{1,0:T(8,128)(2,1)S(1)} %get-tuple-element.46), channel_id=1, source_target_pairs={{0,1},{1,2},{2,3},{3,0},{4,5},{5,6},{6,7},{7,4},{8,9},{9,10},{10,1... | collective-permute-start | bytes 491528 | tf_op jit(solution)/shard_map/ppermute | solution.py:24
  88.9 10.3 %collective-permute-start.9 = (bf16[64,1280]{1,0:T(8,128)(2,1)S(1)}, bf16[64,1280]{1,0:T(8,128)(2,1)S(1)}, u32[]{:S(2)}, u32[]{:S(2)}) collective-permute-start(bf16[64,1280]{1,0:T(8,128)(2,1)S(1)} %get-tuple-element.49), channel_id=1, source_target_pairs={{0,3},{1,0},{2,1},{3,2},{4,7},{5,4},{6,5},{7,6},{8,11},{9,8},{10,9... | collective-permute-start | bytes 491528 | tf_op jit(solution)/shard_map/ppermute | solution.py:24
  92.9 7.9 %collective-permute-start.18 = (bf16[64,1280]{1,0:T(8,128)(2,1)S(1)}, bf16[64,1280]{1,0:T(8,128)(2,1)S(1)}, u32[]{:S(2)}, u32[]{:S(2)}) collective-permute-start(bf16[64,1280]{1,0:T(8,128)(2,1)S(1)} %get-tuple-element.58), channel_id=1, source_target_pairs={{0,1},{1,2},{2,3},{3,0},{4,5},{5,6},{6,7},{7,4},{8,9},{9,10},{10,1... | collective-permute-start | bytes 491528 | tf_op jit(solution)/shard_map/ppermute | solution.py:24
  93.0 7.9 %collective-permute-start.19 = (bf16[64,1280]{1,0:T(8,128)(2,1)S(1)}, bf16[64,1280]{1,0:T(8,128)(2,1)S(1)}, u32[]{:S(2)}, u32[]{:S(2)}) collective-permute-start(bf16[64,1280]{1,0:T(8,128)(2,1)S(1)} %get-tuple-element.59), channel_id=1, source_target_pairs={{0,3},{1,0},{2,1},{3,2},{4,7},{5,4},{6,5},{7,6},{8,11},{9,8},{10,9... | collective-permute-start | bytes 491528 | tf_op jit(solution)/shard_map/ppermute | solution.py:24
  96.2 2.3 %copy-start = (bf16[1,128,4096]{2,1,0:T(8,128)(2,1)S(1)}, bf16[1,128,4096]{2,1,0:T(8,128)(2,1)}, u32[]{:S(2)}) copy-start(bf16[1,128,4096]{2,1,0:T(8,128)(2,1)} %param.7) | copy-start | bytes 3145732
  99.1 17.6 %collective-permute-start.25 = (bf16[128,1536]{1,0:T(8,128)(2,1)S(1)}, bf16[128,1536]{1,0:T(8,128)(2,1)S(1)}, u32[]{:S(2)}, u32[]{:S(2)}) collective-permute-start(bf16[128,1536]{1,0:T(8,128)(2,1)S(1)} %shard_map.87), channel_id=1, source_target_pairs={{0,4},{4,8},{8,12},{12,16},{16,20},{20,24},{24,28},{28,32},{32,36}... | collective-permute-start | bytes 1179656 | tf_op jit(solution)/shard_map/ppermute | solution.py:33
  99.7 13.5 %collective-permute-start.17 = (bf16[128,1280]{1,0:T(8,128)(2,1)S(1)}, bf16[128,1280]{1,0:T(8,128)(2,1)S(1)}, u32[]{:S(2)}, u32[]{:S(2)}) collective-permute-start(bf16[128,1280]{1,0:T(8,128)(2,1)S(1)} %shard_map.84), channel_id=1, source_target_pairs={{0,4},{4,8},{8,12},{12,16},{16,20},{20,24},{24,28},{28,32},{32,36}... | collective-permute-start | bytes 983048 | tf_op jit(solution)/shard_map/ppermute | solution.py:33
  101.4 15.3 %collective-permute-start.20 = (bf16[128,1280]{1,0:T(8,128)(2,1)S(1)}, bf16[128,1280]{1,0:T(8,128)(2,1)S(1)}, u32[]{:S(2)}, u32[]{:S(2)}) collective-permute-start(bf16[128,1280]{1,0:T(8,128)(2,1)S(1)} %shard_map.85), channel_id=1, source_target_pairs={{0,4},{4,8},{8,12},{12,16},{16,20},{20,24},{24,28},{28,32},{32,36}... | collective-permute-start | bytes 983048 | tf_op jit(solution)/shard_map/ppermute | solution.py:33

commit v3 on v2

--- a/solution.py
+++ b/solution.py
@@ -49,12 +49,12 @@
     )(*args)
 
 
-def prologue_kernel(tokens, history, out, early, far, rows_ref, sems):
+def prologue_kernel(tokens, history, out, early, rows_ref, sems):
     token_copy = pltpu.make_async_copy(tokens, rows_ref, sems.at[0])
     token_copy.start()
     copies = [
         pltpu.make_async_copy(history.at[slot - 1], block, sems.at[1 + i])
-        for i, (slot, block) in enumerate(zip(first_slots(), (early, far)))
+        for i, (slot, block) in enumerate(zip(first_slots()[:1], (early,)))
     ]
     for copy in copies:
         copy.start()
@@ -97,7 +97,7 @@
 def slots_kernel(history, *refs):
     outs, sems = refs[:-1], refs[-1]
     _, _, low = place_in_grid()
-    slots = (jnp.where(low, 3, 1), 6, 4, 2, 1)
+    slots = (first_slots()[1], jnp.where(low, 3, 1), 6, 4, 2, 1)
     copies = [
         pltpu.make_async_copy(history.at[slot - 1], out, sems.at[i])
         for i, (slot, out) in enumerate(zip(slots, outs))
@@ -268,6 +268,40 @@
     return kernel
 
 
+def store_kernel(*refs):
+    *pieces, out, sems = refs
+    first, copies = 0, []
+    for i, piece in enumerate(pieces):
+        last = first + piece.shape[1]
+        copies.append(pltpu.make_async_copy(piece, out.at[:, first:last], sems.at[i]))
+        first = last
+    for copy in copies:
+        copy.start()
+    for copy in copies:
+        copy.wait()
+
+
+def store_last_kernel(_, piece, out, sems):
+    copy = pltpu.make_async_copy(piece, out.at[:, out.shape[1] - piece.shape[1] :], sems.at[0])
+    copy.start()
+    copy.wait()
+
+
+def stored(kernel, out, *pieces, aliases):
+    specs = [pl.BlockSpec(memory_space=pltpu.VMEM)] * len(pieces)
+    if aliases:
+        specs[0] = pl.BlockSpec(memory_space=pltpu.HBM)
+    return pl.pallas_call(
+        kernel,
+        out_shape=pltpu.HBM(*out),
+        in_specs=specs,
+        out_specs=pl.BlockSpec(memory_space=pltpu.HBM),
+        scratch_shapes=[pltpu.SemaphoreType.DMA((len(pieces),))],
+        input_output_aliases=aliases,
+        compiler_params=pltpu.CompilerParams(vmem_limit_bytes=4 * MIB),
+    )(*pieces)
+
+
 def cut(width, proportions):
     return [width * part // sum(proportions) for part in proportions]
 
@@ -285,17 +319,17 @@
     rows_of = lambda first, last: range(first * ROW, last * ROW)
     swap = lambda i: DILATION_STRIDE if i % ROW < DILATION_STRIDE else -DILATION_STRIDE
 
-    normed, early, far = on_chip(
-        prologue_kernel, [block] * 3, token_rows, history[0], limit=6,
-        scratch=[pltpu.VMEM((rows, width), BF16), pltpu.SemaphoreType.DMA((3,))], spaces=[pltpu.HBM] * 2,
+    normed, early = on_chip(
+        prologue_kernel, [block] * 2, token_rows, history[0], limit=6,
+        scratch=[pltpu.VMEM((rows, width), BF16), pltpu.SemaphoreType.DMA((2,))], spaces=[pltpu.HBM] * 2,
     )
     left, right = around(normed, 1), around(normed, -1)
     opposite_top, opposite_bottom = around(left[:half], 1), around(right[half:], -1)
 
     pieces_of = [((rows, size), BF16) for size in sizes]
-    late, far_straight, two_straight, one_straight, same_row = on_chip(
-        slots_kernel, [block] * 5, history[0],
-        limit=6, scratch=[pltpu.SemaphoreType.DMA((5,))], spaces=[pltpu.HBM],
+    far, late, far_straight, two_straight, one_straight, same_row = on_chip(
+        slots_kernel, [block] * 6, history[0],
+        limit=7, scratch=[pltpu.SemaphoreType.DMA((6,))], spaces=[pltpu.HBM],
     )
     crossed_early = sent(early, rows_of(0, 3), swap)
     far_odd = sent(far, rows_of(0, 1), lambda i: 3 * ROW + swap(i))
@@ -351,7 +385,8 @@
         )
         pieces.append(to_next_section(mixed))
         first += size
-    return jnp.concatenate(pieces, axis=1)[None]
+    begun = stored(store_kernel, block, *pieces[:-1], aliases={})
+    return stored(store_last_kernel, block, begun, pieces[-1], aliases={0: 0})[None]
 
 
 def solution(mesh):

time: 118 us -> 134 us (1.14)
  waiting for transfers between devices: 36.6 us -> 56.9 us
  starting transfers between devices: 56.5 us -> 52 us
  Pallas kernels: 23.1 us -> 24.6 us
    ppermute x9, waiting for transfers between devices: 3.69 us -> 19.9 us  [sent(): return lax.ppermute(value, 'section', [(i, i + steps(i)) for i in sources])]
    ppermute x14, waiting for transfers between devices: 17.7 us -> 21.7 us  [around(): lax.ppermute(value, 'tensor', [(i, (i + steps) % count) for i in range(co...]
    ppermute x9, starting transfers between devices: 32.5 us -> 28.7 us  [sent(): return lax.ppermute(value, 'section', [(i, i + steps(i)) for i in sources])]
    pallas_call x0 -> x2, Pallas kernels: none -> 1.62 us  [stored(): pl.pallas_call(kernel, out_shape=pltpu.HBM(*out), in_specs=specs, out_spe...]
  transfers between devices with their start and end apart: 26 -> 26, of which waited for: 9 -> 10; matrix products, arithmetic and copies ran while one was open for 0% -> 0% of each run, Pallas kernels for 18% -> 17%
where the time goes in v3:
time: 134 us
  waiting for transfers between devices  56.9 us (42%)
  starting transfers between devices  52 us (39%)
  Pallas kernels  24.6 us (18%)
    ppermute x9, starting transfers between devices, sent(): return lax.ppermute(value, 'section', [(i, i + steps(i)) for i in sources])  28.7 us
    pallas_call x15, Pallas kernels, on_chip(): pl.pallas_call(body, out_shape=[pltpu.VMEM(shape, dtype) for shape, dtype...  23 us
    ppermute x14, starting transfers between devices, around(): lax.ppermute(value, 'tensor', [(i, (i + steps) % count) for i in range(co...  21.9 us
    ppermute x14, waiting for transfers between devices, around(): lax.ppermute(value, 'tensor', [(i, (i + steps) % count) for i in range(co...  21.7 us
    ppermute x9, waiting for transfers between devices, sent(): return lax.ppermute(value, 'section', [(i, i + steps(i)) for i in sources])  19.9 us
    ppermute x3, waiting for transfers between devices, to_next_section(): lax.ppermute(block, 'section', [(i, (i + 1) % count) for i in range(count)])  15.2 us
  transfers between devices with their start and end apart: 26, of which 10 were waited for; matrix products, arithmetic and copies ran while one was open for 0% of the time, Pallas kernels for 17%

profile of v3, /device:TPU:0, one launch (start us, length us, event | category | flops | bytes accessed | tf_op | source)
XLA Modules:
  0.0 134.1 jit_solution(9518091645926057578)
XLA Ops:
  0.0 1.6 %shard_map.73 = (bf16[128,4096]{1,0:T(8,128)(2,1)S(1)}, bf16[128,4096]{1,0:T(8,128)(2,1)S(1)}) custom-call(bf16[128,4096]{1,0:T(8,128)(2,1)} %bitcast.18, bf16[7,128,4096]{2,1,0:T(8,128)(2,1)} %bitcast.28), custom_call_target="tpu_custom_call" | custom-call | tf_op jit(solution)/shard_map/pallas_call | solution.py:42
  1.6 2.9 %collective-permute-start.1 = (bf16[128,4096]{1,0:T(8,128)(2,1)S(1)}, bf16[128,4096]{1,0:T(8,128)(2,1)S(1)}, u32[]{:S(2)}, u32[]{:S(2)}) collective-permute-start(bf16[128,4096]{1,0:T(8,128)(2,1)S(1)} %get-tuple-element.34.refs_0_), channel_id=1, source_target_pairs={{0,3},{1,0},{2,1},{3,2},{4,7},{5,4},{6,5},{7,6},{8,11},{9,8},{10,9... | collective-permute-start | bytes 3145736 | tf_op jit(solution)/shard_map/ppermute | solution.py:24
  4.6 6.0 %collective-permute-start.10 = (bf16[128,4096]{1,0:T(8,128)(2,1)S(1)}, bf16[128,4096]{1,0:T(8,128)(2,1)S(1)}, u32[]{:S(2)}, u32[]{:S(2)}) collective-permute-start(bf16[128,4096]{1,0:T(8,128)(2,1)S(1)} %get-tuple-element.51), channel_id=1, source_target_pairs={{0,16},{4,20},{8,24},{12,28},{16,0},{20,4},{24,8},{28,12},{32,48},... | collective-permute-start | bytes 3145736 | tf_op jit(solution)/shard_map/ppermute | solution.py:28
  10.6 2.9 %shard_map.81 = (bf16[128,4096]{1,0:T(8,128)(2,1)S(1)}, bf16[128,4096]{1,0:T(8,128)(2,1)S(1)}, bf16[128,4096]{1,0:T(8,128)(2,1)S(1)}, bf16[128,4096]{1,0:T(8,128...) custom-call(bf16[7,128,4096]{2,1,0:T(8,128)(2,1)} %bitcast.29), custom_call_target="tpu_custom_call" | custom-call | tf_op jit(solution)/shard_map/pallas_call | solution.py:42
  13.5 2.0 %collective-permute-start.11 = (bf16[128,4096]{1,0:T(8,128)(2,1)S(1)}, bf16[128,4096]{1,0:T(8,128)(2,1)S(1)}, u32[]{:S(2)}, u32[]{:S(2)}) collective-permute-start(bf16[128,4096]{1,0:T(8,128)(2,1)S(1)} %get-tuple-element.52), channel_id=1, source_target_pairs={{0,16},{4,20},{8,24},{12,28},{16,0},{20,4},{24,8},{28,12},{32,48},... | collective-permute-start | bytes 3145736 | tf_op jit(solution)/shard_map/ppermute | solution.py:28
  15.5 1.5 %collective-permute-start.14 = (bf16[128,4096]{1,0:T(8,128)(2,1)S(1)}, bf16[128,4096]{1,0:T(8,128)(2,1)S(1)}, u32[]{:S(2)}, u32[]{:S(2)}) collective-permute-start(bf16[128,4096]{1,0:T(8,128)(2,1)S(1)} %get-tuple-element.55), channel_id=1, source_target_pairs={{0,96},{4,100},{8,104},{12,108},{16,112},{20,116},{24,120},{28,124... | collective-permute-start | bytes 3145736 | tf_op jit(solution)/shard_map/ppermute | solution.py:28
  17.0 10.0 %collective-permute-done.1.refs_1_ = bf16[128,4096]{1,0:T(8,128)(2,1)S(1)} collective-permute-done((bf16[128,4096]{1,0:T(8,128)(2,1)S(1)}, bf16[128,4096]{1,0:T(8,128)(2,1)S(1)}, u32[]{:S(2)}, u32[]{:S(2)}) %collective-permute-start.1) | collective-permute-done | bytes 1048608 | tf_op jit(solution)/shard_map/ppermute | solution.py:24
  27.0 3.8 %collective-permute-start.3 = (bf16[64,4096]{1,0:T(8,128)(2,1)S(1)}, bf16[64,4096]{1,0:T(8,128)(2,1)S(1)}, u32[]{:S(2)}, u32[]{:S(2)}) collective-permute-start(bf16[64,4096]{1,0:T(8,128)(2,1)S(1)} %slice.9), channel_id=1, source_target_pairs={{0,3},{1,0},{2,1},{3,2},{4,7},{5,4},{6,5},{7,6},{8,11},{9,8},{10,9... | collective-permute-start | bytes 1572872 | tf_op jit(solution)/shard_map/ppermute | solution.py:24
  30.9 3.7 %collective-permute-done.10.crossed.crossed_early = bf16[128,4096]{1,0:T(8,128)(2,1)S(1)} collective-permute-done((bf16[128,4096]{1,0:T(8,128)(2,1)S(1)}, bf16[128,4096]{1,0:T(8,128)(2,1)S(1)}, u32[]{:S(2)}, u32[]{:S(2)}) %collective-permute-start.10) | collective-permute-done | bytes 1048608 | tf_op jit(solution)/shard_map/ppermute | solution.py:28
  34.6 4.6 %collective-permute-start.15 = (bf16[128,4096]{1,0:T(8,128)(2,1)S(1)}, bf16[128,4096]{1,0:T(8,128)(2,1)S(1)}, u32[]{:S(2)}, u32[]{:S(2)}) collective-permute-start(bf16[128,4096]{1,0:T(8,128)(2,1)S(1)} %get-tuple-element.56), channel_id=1, source_target_pairs={{0,112},{4,116},{8,120},{12,124},{16,96},{20,100},{24,104},{28,108... | collective-permute-start | bytes 3145736 | tf_op jit(solution)/shard_map/ppermute | solution.py:28
  39.2 0.5 shard_map.82
  39.7 16.2 %collective-permute-done.11.crossed_late = bf16[128,4096]{1,0:T(8,128)(2,1)S(1)} collective-permute-done((bf16[128,4096]{1,0:T(8,128)(2,1)S(1)}, bf16[128,4096]{1,0:T(8,128)(2,1)S(1)}, u32[]{:S(2)}, u32[]{:S(2)}) %collective-permute-start.11) | collective-permute-done | bytes 1048608 | tf_op jit(solution)/shard_map/ppermute | solution.py:28
  56.0 3.5 %collective-permute-start.23 = (bf16[128,1536]{1,0:T(8,128)(2,1)S(1)}, bf16[128,1536]{1,0:T(8,128)(2,1)S(1)}, u32[]{:S(2)}, u32[]{:S(2)}) collective-permute-start(bf16[128,1536]{1,0:T(8,128)(2,1)S(1)} %get-tuple-element.62), channel_id=1, source_target_pairs={{0,32},{4,36},{8,40},{12,44},{16,48},{20,52},{24,56},{28,60},{32,6... | collective-permute-start | bytes 1179656 | tf_op jit(solution)/shard_map/ppermute | solution.py:28
  59.5 5.2 %collective-permute-start.16 = (bf16[128,4096]{1,0:T(8,128)(2,1)S(1)}, bf16[128,4096]{1,0:T(8,128)(2,1)S(1)}, u32[]{:S(2)}, u32[]{:S(2)}) collective-permute-start(bf16[128,4096]{1,0:T(8,128)(2,1)S(1)} %get-tuple-element.57), channel_id=1, source_target_pairs={{0,16},{4,20},{8,24},{12,28},{32,48},{36,52},{40,56},{44,60},{64,8... | collective-permute-start | bytes 3145736 | tf_op jit(solution)/shard_map/ppermute | solution.py:28
  64.7 1.9 %collective-permute-start.12 = (bf16[128,2560]{1,0:T(8,128)(2,1)S(1)}, bf16[128,2560]{1,0:T(8,128)(2,1)S(1)}, u32[]{:S(2)}, u32[]{:S(2)}) collective-permute-start(bf16[128,2560]{1,0:T(8,128)(2,1)S(1)} %get-tuple-element.54), channel_id=1, source_target_pairs={{0,32},{4,36},{8,40},{12,44},{16,48},{20,52},{24,56},{28,60},{32,6... | collective-permute-start | bytes 1966088 | tf_op jit(solution)/shard_map/ppermute | solution.py:28
  66.6 1.6 %shard_map.74.refs_2_.refs_3_.joined = bf16[4096,256]{1,0:T(8,128)(2,1)S(1)} custom-call(bf16[4096,128]{1,0:T(8,128)(2,1)} %bitcast.30, bf16[4096,128]{1,0:T(8,128)(2,1)} %bitcast.31), custom_call_target="tpu_custom_call" | custom-call | tf_op jit(solution)/shard_map/pallas_call | solution.py:42
  68.3 1.3 shard_map.75
  69.6 2.4 %shard_map.76 = (bf16[256,768]{1,0:T(8,128)(2,1)S(1)}, bf16[256,1024]{1,0:T(8,128)(2,1)S(1)}) custom-call(bf16[128,4096]{1,0:T(8,128)(2,1)S(1)} %collective-permute-done.refs_0_, bf16[128,4096]{1,0:T(8,128)(2,1)S(1)} %collective-permute-done.1.refs_1_, bf16[4096,768]{1,0:T(8,128)(2,1)S(1)} %bitcast.11, bf16[4096,256]{1,0:T(8,128)(2,1)S(1)} %shard_map.74.refs_2_.refs_3_.joined), custom_call_target="tpu_custom_call" | custom-call | tf_op jit(solution)/shard_map/pallas_call | solution.py:42
  72.0 3.4 %shard_map.77 = (bf16[64,4096]{1,0:T(8,128)(2,1)S(1)}, bf16[64,4096]{1,0:T(8,128)(2,1)S(1)}, bf16[128,1024]{1,0:T(8,128)(2,1)S(1)}) custom-call(bf16[64,4096]{1,0:T(8,128)(2,1)S(1)} %collective-permute-done.2.top, bf16[64,4096]{1,0:T(8,128)(2,1)S(1)} %collective-permute-done.3.bottom, bf16[4096,768]{1,0:T(8,128)(2,1)S(1)} %bitcast.12, ...), custom_call_target="tpu_custom_call" | custom-call | tf_op jit(solution)/shard_map/pallas_call | solution.py:42
  75.5 0.5 collective-permute-start.5
  76.0 2.8 %collective-permute-start.6 = (bf16[64,4096]{1,0:T(8,128)(2,1)S(1)}, bf16[64,4096]{1,0:T(8,128)(2,1)S(1)}, u32[]{:S(2)}, u32[]{:S(2)}) collective-permute-start(bf16[64,4096]{1,0:T(8,128)(2,1)S(1)} %get-tuple-element.45), channel_id=1, source_target_pairs={{0,3},{1,0},{2,1},{3,2},{4,7},{5,4},{6,5},{7,6},{8,11},{9,8},{10,9... | collective-permute-start | bytes 1572872 | tf_op jit(solution)/shard_map/ppermute | solution.py:24
  78.8 0.4 shard_map.87
  79.2 2.1 %collective-permute-start.24 = (bf16[128,1536]{1,0:T(8,128)(2,1)S(1)}, bf16[128,1536]{1,0:T(8,128)(2,1)S(1)}, u32[]{:S(2)}, u32[]{:S(2)}) collective-permute-start(bf16[128,1536]{1,0:T(8,128)(2,1)S(1)} %shard_map.87), channel_id=1, source_target_pairs={{0,32},{4,36},{8,40},{12,44},{16,48},{20,52},{24,56},{28,60},{32,6... | collective-permute-start | bytes 1179656 | tf_op jit(solution)/shard_map/ppermute | solution.py:28
  81.3 4.2 %shard_map.79 = (bf16[64,4096]{1,0:T(8,128)(2,1)S(1)}, bf16[64,4096]{1,0:T(8,128)(2,1)S(1)}, bf16[64,4096]{1,0:T(8,128)(2,1)S(1)}, bf16[64,4096]{1,0:T(8,128)(2,1)S(1)}) custom-call(bf16[256,768]{1,0:T(8,128)(2,1)S(1)} %get-tuple-element.40.query, bf16[128,1024]{1,0:T(8,128)(2,1)S(1)} %get-tuple-element.36.kv0, bf16[256,1024]{1,0:T(8,128)(2,1)S(1)} %get-tuple-element.37.kv1, ...), custom_call_target="tpu_custom_call" | custom-call | tf_op jit(solution)/shard_map/pallas_call | solution.py:42
  85.5 1.8 %collective-permute-start.4 = (bf16[64,4096]{1,0:T(8,128)(2,1)S(1)}, bf16[64,4096]{1,0:T(8,128)(2,1)S(1)}, u32[]{:S(2)}, u32[]{:S(2)}) collective-permute-start(bf16[64,4096]{1,0:T(8,128)(2,1)S(1)} %get-tuple-element.41), channel_id=1, source_target_pairs={{0,3},{1,0},{2,1},{3,2},{4,7},{5,4},{6,5},{7,6},{8,11},{9,8},{10,9... | collective-permute-start | bytes 1572872 | tf_op jit(solution)/shard_map/ppermute | solution.py:24
  87.3 1.4 %collective-permute-done.5.from_left = bf16[64,4096]{1,0:T(8,128)(2,1)S(1)} collective-permute-done((bf16[64,4096]{1,0:T(8,128)(2,1)S(1)}, bf16[64,4096]{1,0:T(8,128)(2,1)S(1)}, u32[]{:S(2)}, u32[]{:S(2)}) %collective-permute-start.5) | collective-permute-done | bytes 524320 | tf_op jit(solution)/shard_map/ppermute | solution.py:24
  88.7 0.6 shard_map.83
  89.3 1.8 %collective-permute-done.6.from_right = bf16[64,4096]{1,0:T(8,128)(2,1)S(1)} collective-permute-done((bf16[64,4096]{1,0:T(8,128)(2,1)S(1)}, bf16[64,4096]{1,0:T(8,128)(2,1)S(1)}, u32[]{:S(2)}, u32[]{:S(2)}) %collective-permute-start.6) | collective-permute-done | bytes 524320 | tf_op jit(solution)/shard_map/ppermute | solution.py:24
  91.1 1.9 %collective-permute-start.13 = (bf16[128,2560]{1,0:T(8,128)(2,1)S(1)}, bf16[128,2560]{1,0:T(8,128)(2,1)S(1)}, u32[]{:S(2)}, u32[]{:S(2)}) collective-permute-start(bf16[128,2560]{1,0:T(8,128)(2,1)S(1)} %shard_map.83), channel_id=1, source_target_pairs={{0,32},{4,36},{8,40},{12,44},{16,48},{20,52},{24,56},{28,60},{32,6... | collective-permute-start | bytes 1966088 | tf_op jit(solution)/shard_map/ppermute | solution.py:28
  93.0 0.2 shard_map.80
  93.3 1.7 %collective-permute-start.21 = (bf16[64,1536]{1,0:T(8,128)(2,1)S(1)}, bf16[64,1536]{1,0:T(8,128)(2,1)S(1)}, u32[]{:S(2)}, u32[]{:S(2)}) collective-permute-start(bf16[64,1536]{1,0:T(8,128)(2,1)S(1)} %get-tuple-element.60), channel_id=1, source_target_pairs={{0,1},{1,2},{2,3},{3,0},{4,5},{5,6},{6,7},{7,4},{8,9},{9,10},{10,1... | collective-permute-start | bytes 589832 | tf_op jit(solution)/shard_map/ppermute | solution.py:24
  94.9 2.2 %collective-permute-start.22 = (bf16[64,1536]{1,0:T(8,128)(2,1)S(1)}, bf16[64,1536]{1,0:T(8,128)(2,1)S(1)}, u32[]{:S(2)}, u32[]{:S(2)}) collective-permute-start(bf16[64,1536]{1,0:T(8,128)(2,1)S(1)} %get-tuple-element.61), channel_id=1, source_target_pairs={{0,3},{1,0},{2,1},{3,2},{4,7},{5,4},{6,5},{7,6},{8,11},{9,8},{10,9... | collective-permute-start | bytes 589832 | tf_op jit(solution)/shard_map/ppermute | solution.py:24
  97.1 5.2 %collective-permute-done.4.refs_1_ = bf16[64,4096]{1,0:T(8,128)(2,1)S(1)} collective-permute-done((bf16[64,4096]{1,0:T(8,128)(2,1)S(1)}, bf16[64,4096]{1,0:T(8,128)(2,1)S(1)}, u32[]{:S(2)}, u32[]{:S(2)}) %collective-permute-start.4) | collective-permute-done | bytes 524320 | tf_op jit(solution)/shard_map/ppermute | solution.py:24
  102.3 1.6 %collective-permute-start.7 = (bf16[64,1280]{1,0:T(8,128)(2,1)S(1)}, bf16[64,1280]{1,0:T(8,128)(2,1)S(1)}, u32[]{:S(2)}, u32[]{:S(2)}) collective-permute-start(bf16[64,1280]{1,0:T(8,128)(2,1)S(1)} %get-tuple-element.46), channel_id=1, source_target_pairs={{0,1},{1,2},{2,3},{3,0},{4,5},{5,6},{6,7},{7,4},{8,9},{9,10},{10,1... | collective-permute-start | bytes 491528 | tf_op jit(solution)/shard_map/ppermute | solution.py:24
  103.9 0.8 collective-permute-done.8.refs_4_
  104.7 1.3 collective-permute-start.9
  106.0 2.5 %collective-permute-done.21.refs_2_ = bf16[64,1536]{1,0:T(8,128)(2,1)S(1)} collective-permute-done((bf16[64,1536]{1,0:T(8,128)(2,1)S(1)}, bf16[64,1536]{1,0:T(8,128)(2,1)S(1)}, u32[]{:S(2)}, u32[]{:S(2)}) %collective-permute-start.21) | collective-permute-done | bytes 196640 | tf_op jit(solution)/shard_map/ppermute | solution.py:24
  108.5 3.2 %collective-permute-start.19 = (bf16[64,1280]{1,0:T(8,128)(2,1)S(1)}, bf16[64,1280]{1,0:T(8,128)(2,1)S(1)}, u32[]{:S(2)}, u32[]{:S(2)}) collective-permute-start(bf16[64,1280]{1,0:T(8,128)(2,1)S(1)} %get-tuple-element.59), channel_id=1, source_target_pairs={{0,3},{1,0},{2,1},{3,2},{4,7},{5,4},{6,5},{7,6},{8,11},{9,8},{10,9... | collective-permute-start | bytes 491528 | tf_op jit(solution)/shard_map/ppermute | solution.py:24
  111.8 2.2 %shard_map.78 = (bf16[64,4096]{1,0:T(8,128)(2,1)S(1)}, bf16[64,4096]{1,0:T(8,128)(2,1)S(1)}) custom-call(bf16[128,768]{1,0:T(8,128)(2,1)S(1)} %get-tuple-element.35.query, bf16[128,1024]{1,0:T(8,128)(2,1)S(1)} %get-tuple-element.36.kv0, bf16[256,1024]{1,0:T(8,128)(2,1)S(1)} %get-tuple-element.37.kv1, bf16[128,1024]{1,0:T(8,128)(2,1)S(1)} %get-tuple-element.38.kv3, ...), custom_call_target="tpu_custom_call" | custom-call | tf_op jit(solution)/shard_map/pallas_call | solution.py:42
  114.0 0.6 shard_map.88
  114.8 0.5 shard_map.84
  115.3 1.2 collective-permute-start.17
  116.4 0.5 shard_map.85
  117.0 0.1 collective-permute-start.20
  117.1 11.7 %collective-permute-done.17.refs_0_ = bf16[128,1280]{1,0:T(8,128)(2,1)S(1)} collective-permute-done((bf16[128,1280]{1,0:T(8,128)(2,1)S(1)}, bf16[128,1280]{1,0:T(8,128)(2,1)S(1)}, u32[]{:S(2)}, u32[]{:S(2)}) %collective-permute-start.17) | collective-permute-done | bytes 327712 | tf_op jit(solution)/shard_map/ppermute | solution.py:33
  128.8 3.5 %collective-permute-done.20.refs_1_ = bf16[128,1280]{1,0:T(8,128)(2,1)S(1)} collective-permute-done((bf16[128,1280]{1,0:T(8,128)(2,1)S(1)}, bf16[128,1280]{1,0:T(8,128)(2,1)S(1)}, u32[]{:S(2)}, u32[]{:S(2)}) %collective-permute-start.20) | collective-permute-done | bytes 327712 | tf_op jit(solution)/shard_map/ppermute | solution.py:33
  132.3 0.8 shard_map.86._
  133.1 0.8 shard_map.89
  (37 shorter events, 0.3 us)
Async XLA Ops:
  1.6 37.6 %copy-start.1 = (f32[32,8]{0,1:T(8,128)S(1)}, f32[32,8]{0,1:T(8,128)}, u32[]{:S(2)}) copy-start(f32[32,8]{0,1:T(8,128)} %param.13) | copy-start | bytes 3076
  1.6 25.4 %collective-permute-start.1 = (bf16[128,4096]{1,0:T(8,128)(2,1)S(1)}, bf16[128,4096]{1,0:T(8,128)(2,1)S(1)}, u32[]{:S(2)}, u32[]{:S(2)}) collective-permute-start(bf16[128,4096]{1,0:T(8,128)(2,1)S(1)} %get-tuple-element.34.refs_0_), channel_id=1, source_target_pairs={{0,3},{1,0},{2,1},{3,2},{4,7},{5,4},{6,5},{7,6},{8,11},{9,8},{10,9... | collective-permute-start | bytes 3145736 | tf_op jit(solution)/shard_map/ppermute | solution.py:24
  4.6 26.2 %collective-permute-start = (bf16[128,4096]{1,0:T(8,128)(2,1)S(1)}, bf16[128,4096]{1,0:T(8,128)(2,1)S(1)}, u32[]{:S(2)}, u32[]{:S(2)}) collective-permute-start(bf16[128,4096]{1,0:T(8,128)(2,1)S(1)} %get-tuple-element.34.refs_0_), channel_id=1, source_target_pairs={{0,1},{1,2},{2,3},{3,0},{4,5},{5,6},{6,7},{7,4},{8,9},{9,10},{10,1... | collective-permute-start | bytes 3145736 | tf_op jit(solution)/shard_map/ppermute | solution.py:24
  4.6 63.6 %slice-start = ((s8[6291456]{0:T(1024)(128)(4,1)}), s8[4194304]{0:T(1024)(128)(4,1)S(1)}, s32[]{:S(2)}) async-start(s8[6291456]{0:T(1024)(128)(4,1)} %bitcast.8), calls=%async_computation | async-start | bytes 8388608
  4.6 30.0 %collective-permute-start.10 = (bf16[128,4096]{1,0:T(8,128)(2,1)S(1)}, bf16[128,4096]{1,0:T(8,128)(2,1)S(1)}, u32[]{:S(2)}, u32[]{:S(2)}) collective-permute-start(bf16[128,4096]{1,0:T(8,128)(2,1)S(1)} %get-tuple-element.51), channel_id=1, source_target_pairs={{0,16},{4,20},{8,24},{12,28},{16,0},{20,4},{24,8},{28,12},{32,48},... | collective-permute-start | bytes 3145736 | tf_op jit(solution)/shard_map/ppermute | solution.py:28
  13.5 42.5 %collective-permute-start.11 = (bf16[128,4096]{1,0:T(8,128)(2,1)S(1)}, bf16[128,4096]{1,0:T(8,128)(2,1)S(1)}, u32[]{:S(2)}, u32[]{:S(2)}) collective-permute-start(bf16[128,4096]{1,0:T(8,128)(2,1)S(1)} %get-tuple-element.52), channel_id=1, source_target_pairs={{0,16},{4,20},{8,24},{12,28},{16,0},{20,4},{24,8},{28,12},{32,48},... | collective-permute-start | bytes 3145736 | tf_op jit(solution)/shard_map/ppermute | solution.py:28
  15.5 52.7 %slice-start.1 = ((s8[6291456]{0:T(1024)(128)(4,1)}), s8[2097152]{0:T(1024)(128)(4,1)S(1)}, s32[]{:S(2)}) async-start(s8[6291456]{0:T(1024)(128)(4,1)} %bitcast.8), calls=%async_computation.1 | async-start | bytes 4194304
  15.5 60.0 %collective-permute-start.14 = (bf16[128,4096]{1,0:T(8,128)(2,1)S(1)}, bf16[128,4096]{1,0:T(8,128)(2,1)S(1)}, u32[]{:S(2)}, u32[]{:S(2)}) collective-permute-start(bf16[128,4096]{1,0:T(8,128)(2,1)S(1)} %get-tuple-element.55), channel_id=1, source_target_pairs={{0,96},{4,100},{8,104},{12,108},{16,112},{20,116},{24,120},{28,124... | collective-permute-start | bytes 3145736 | tf_op jit(solution)/shard_map/ppermute | solution.py:28
  27.0 32.4 %collective-permute-start.3 = (bf16[64,4096]{1,0:T(8,128)(2,1)S(1)}, bf16[64,4096]{1,0:T(8,128)(2,1)S(1)}, u32[]{:S(2)}, u32[]{:S(2)}) collective-permute-start(bf16[64,4096]{1,0:T(8,128)(2,1)S(1)} %slice.9), channel_id=1, source_target_pairs={{0,3},{1,0},{2,1},{3,2},{4,7},{5,4},{6,5},{7,6},{8,11},{9,8},{10,9... | collective-permute-start | bytes 1572872 | tf_op jit(solution)/shard_map/ppermute | solution.py:24
  30.8 33.9 %collective-permute-start.2 = (bf16[64,4096]{1,0:T(8,128)(2,1)S(1)}, bf16[64,4096]{1,0:T(8,128)(2,1)S(1)}, u32[]{:S(2)}, u32[]{:S(2)}) collective-permute-start(bf16[64,4096]{1,0:T(8,128)(2,1)S(1)} %slice.8), channel_id=1, source_target_pairs={{0,1},{1,2},{2,3},{3,0},{4,5},{5,6},{6,7},{7,4},{8,9},{9,10},{10,1... | collective-permute-start | bytes 1572872 | tf_op jit(solution)/shard_map/ppermute | solution.py:24
  34.6 44.6 %collective-permute-start.15 = (bf16[128,4096]{1,0:T(8,128)(2,1)S(1)}, bf16[128,4096]{1,0:T(8,128)(2,1)S(1)}, u32[]{:S(2)}, u32[]{:S(2)}) collective-permute-start(bf16[128,4096]{1,0:T(8,128)(2,1)S(1)} %get-tuple-element.56), channel_id=1, source_target_pairs={{0,112},{4,116},{8,120},{12,124},{16,96},{20,100},{24,104},{28,108... | collective-permute-start | bytes 3145736 | tf_op jit(solution)/shard_map/ppermute | solution.py:28
  56.0 20.1 %collective-permute-start.23 = (bf16[128,1536]{1,0:T(8,128)(2,1)S(1)}, bf16[128,1536]{1,0:T(8,128)(2,1)S(1)}, u32[]{:S(2)}, u32[]{:S(2)}) collective-permute-start(bf16[128,1536]{1,0:T(8,128)(2,1)S(1)} %get-tuple-element.62), channel_id=1, source_target_pairs={{0,32},{4,36},{8,40},{12,44},{16,48},{20,52},{24,56},{28,60},{32,6... | collective-permute-start | bytes 1179656 | tf_op jit(solution)/shard_map/ppermute | solution.py:28
  59.5 33.8 %collective-permute-start.16 = (bf16[128,4096]{1,0:T(8,128)(2,1)S(1)}, bf16[128,4096]{1,0:T(8,128)(2,1)S(1)}, u32[]{:S(2)}, u32[]{:S(2)}) collective-permute-start(bf16[128,4096]{1,0:T(8,128)(2,1)S(1)} %get-tuple-element.57), channel_id=1, source_target_pairs={{0,16},{4,20},{8,24},{12,28},{32,48},{36,52},{40,56},{44,60},{64,8... | collective-permute-start | bytes 3145736 | tf_op jit(solution)/shard_map/ppermute | solution.py:28
  64.7 20.8 %collective-permute-start.12 = (bf16[128,2560]{1,0:T(8,128)(2,1)S(1)}, bf16[128,2560]{1,0:T(8,128)(2,1)S(1)}, u32[]{:S(2)}, u32[]{:S(2)}) collective-permute-start(bf16[128,2560]{1,0:T(8,128)(2,1)S(1)} %get-tuple-element.54), channel_id=1, source_target_pairs={{0,32},{4,36},{8,40},{12,44},{16,48},{20,52},{24,56},{28,60},{32,6... | collective-permute-start | bytes 1966088 | tf_op jit(solution)/shard_map/ppermute | solution.py:28
  68.2 3.8 %slice-start.2 = ((s8[6291456]{0:T(1024)(128)(4,1)}), s8[4194304]{0:T(1024)(128)(4,1)S(1)}, s32[]{:S(2)}) async-start(s8[6291456]{0:T(1024)(128)(4,1)} %bitcast.13), calls=%async_computation.2 | async-start | bytes 8388608
  69.6 2.4 %slice-start.3 = ((s8[6291456]{0:T(1024)(128)(4,1)}), s8[2097152]{0:T(1024)(128)(4,1)S(1)}, s32[]{:S(2)}) async-start(s8[6291456]{0:T(1024)(128)(4,1)} %bitcast.13), calls=%async_computation.3 | async-start | bytes 4194304
  75.5 13.3 %collective-permute-start.5 = (bf16[64,4096]{1,0:T(8,128)(2,1)S(1)}, bf16[64,4096]{1,0:T(8,128)(2,1)S(1)}, u32[]{:S(2)}, u32[]{:S(2)}) collective-permute-start(bf16[64,4096]{1,0:T(8,128)(2,1)S(1)} %get-tuple-element.44), channel_id=1, source_target_pairs={{0,1},{1,2},{2,3},{3,0},{4,5},{5,6},{6,7},{7,4},{8,9},{9,10},{10,1... | collective-permute-start | bytes 1572872 | tf_op jit(solution)/shard_map/ppermute | solution.py:24
  76.0 15.1 %collective-permute-start.6 = (bf16[64,4096]{1,0:T(8,128)(2,1)S(1)}, bf16[64,4096]{1,0:T(8,128)(2,1)S(1)}, u32[]{:S(2)}, u32[]{:S(2)}) collective-permute-start(bf16[64,4096]{1,0:T(8,128)(2,1)S(1)} %get-tuple-element.45), channel_id=1, source_target_pairs={{0,3},{1,0},{2,1},{3,2},{4,7},{5,4},{6,5},{7,6},{8,11},{9,8},{10,9... | collective-permute-start | bytes 1572872 | tf_op jit(solution)/shard_map/ppermute | solution.py:24
  79.2 15.8 %collective-permute-start.24 = (bf16[128,1536]{1,0:T(8,128)(2,1)S(1)}, bf16[128,1536]{1,0:T(8,128)(2,1)S(1)}, u32[]{:S(2)}, u32[]{:S(2)}) collective-permute-start(bf16[128,1536]{1,0:T(8,128)(2,1)S(1)} %shard_map.87), channel_id=1, source_target_pairs={{0,32},{4,36},{8,40},{12,44},{16,48},{20,52},{24,56},{28,60},{32,6... | collective-permute-start | bytes 1179656 | tf_op jit(solution)/shard_map/ppermute | solution.py:28
  85.5 16.8 %collective-permute-start.4 = (bf16[64,4096]{1,0:T(8,128)(2,1)S(1)}, bf16[64,4096]{1,0:T(8,128)(2,1)S(1)}, u32[]{:S(2)}, u32[]{:S(2)}) collective-permute-start(bf16[64,4096]{1,0:T(8,128)(2,1)S(1)} %get-tuple-element.41), channel_id=1, source_target_pairs={{0,3},{1,0},{2,1},{3,2},{4,7},{5,4},{6,5},{7,6},{8,11},{9,8},{10,9... | collective-permute-start | bytes 1572872 | tf_op jit(solution)/shard_map/ppermute | solution.py:24
  88.7 25.3 %copy-start = (bf16[1,128,4096]{2,1,0:T(8,128)(2,1)S(1)}, bf16[1,128,4096]{2,1,0:T(8,128)(2,1)}, u32[]{:S(2)}) copy-start(bf16[1,128,4096]{2,1,0:T(8,128)(2,1)} %param.7) | copy-start | bytes 3145732
  88.7 16.0 %collective-permute-start.8 = (bf16[64,4096]{1,0:T(8,128)(2,1)S(1)}, bf16[64,4096]{1,0:T(8,128)(2,1)S(1)}, u32[]{:S(2)}, u32[]{:S(2)}) collective-permute-start(bf16[64,4096]{1,0:T(8,128)(2,1)S(1)} %get-tuple-element.48), channel_id=1, source_target_pairs={{0,1},{1,2},{2,3},{3,0},{4,5},{5,6},{6,7},{7,4},{8,9},{9,10},{10,1... | collective-permute-start | bytes 1572872 | tf_op jit(solution)/shard_map/ppermute | solution.py:24
  91.1 23.7 %collective-permute-start.13 = (bf16[128,2560]{1,0:T(8,128)(2,1)S(1)}, bf16[128,2560]{1,0:T(8,128)(2,1)S(1)}, u32[]{:S(2)}, u32[]{:S(2)}) collective-permute-start(bf16[128,2560]{1,0:T(8,128)(2,1)S(1)} %shard_map.83), channel_id=1, source_target_pairs={{0,32},{4,36},{8,40},{12,44},{16,48},{20,52},{24,56},{28,60},{32,6... | collective-permute-start | bytes 1966088 | tf_op jit(solution)/shard_map/ppermute | solution.py:28
  93.3 15.3 %collective-permute-start.21 = (bf16[64,1536]{1,0:T(8,128)(2,1)S(1)}, bf16[64,1536]{1,0:T(8,128)(2,1)S(1)}, u32[]{:S(2)}, u32[]{:S(2)}) collective-permute-start(bf16[64,1536]{1,0:T(8,128)(2,1)S(1)} %get-tuple-element.60), channel_id=1, source_target_pairs={{0,1},{1,2},{2,3},{3,0},{4,5},{5,6},{6,7},{7,4},{8,9},{9,10},{10,1... | collective-permute-start | bytes 589832 | tf_op jit(solution)/shard_map/ppermute | solution.py:24
  94.9 13.6 %collective-permute-start.22 = (bf16[64,1536]{1,0:T(8,128)(2,1)S(1)}, bf16[64,1536]{1,0:T(8,128)(2,1)S(1)}, u32[]{:S(2)}, u32[]{:S(2)}) collective-permute-start(bf16[64,1536]{1,0:T(8,128)(2,1)S(1)} %get-tuple-element.61), channel_id=1, source_target_pairs={{0,3},{1,0},{2,1},{3,2},{4,7},{5,4},{6,5},{7,6},{8,11},{9,8},{10,9... | collective-permute-start | bytes 589832 | tf_op jit(solution)/shard_map/ppermute | solution.py:24
  102.3 12.3 %collective-permute-start.7 = (bf16[64,1280]{1,0:T(8,128)(2,1)S(1)}, bf16[64,1280]{1,0:T(8,128)(2,1)S(1)}, u32[]{:S(2)}, u32[]{:S(2)}) collective-permute-start(bf16[64,1280]{1,0:T(8,128)(2,1)S(1)} %get-tuple-element.46), channel_id=1, source_target_pairs={{0,1},{1,2},{2,3},{3,0},{4,5},{5,6},{6,7},{7,4},{8,9},{9,10},{10,1... | collective-permute-start | bytes 491528 | tf_op jit(solution)/shard_map/ppermute | solution.py:24
  104.7 10.0 %collective-permute-start.9 = (bf16[64,1280]{1,0:T(8,128)(2,1)S(1)}, bf16[64,1280]{1,0:T(8,128)(2,1)S(1)}, u32[]{:S(2)}, u32[]{:S(2)}) collective-permute-start(bf16[64,1280]{1,0:T(8,128)(2,1)S(1)} %get-tuple-element.49), channel_id=1, source_target_pairs={{0,3},{1,0},{2,1},{3,2},{4,7},{5,4},{6,5},{7,6},{8,11},{9,8},{10,9... | collective-permute-start | bytes 491528 | tf_op jit(solution)/shard_map/ppermute | solution.py:24
  108.5 7.9 %collective-permute-start.18 = (bf16[64,1280]{1,0:T(8,128)(2,1)S(1)}, bf16[64,1280]{1,0:T(8,128)(2,1)S(1)}, u32[]{:S(2)}, u32[]{:S(2)}) collective-permute-start(bf16[64,1280]{1,0:T(8,128)(2,1)S(1)} %get-tuple-element.58), channel_id=1, source_target_pairs={{0,1},{1,2},{2,3},{3,0},{4,5},{5,6},{6,7},{7,4},{8,9},{9,10},{10,1... | collective-permute-start | bytes 491528 | tf_op jit(solution)/shard_map/ppermute | solution.py:24
  108.5 7.9 %collective-permute-start.19 = (bf16[64,1280]{1,0:T(8,128)(2,1)S(1)}, bf16[64,1280]{1,0:T(8,128)(2,1)S(1)}, u32[]{:S(2)}, u32[]{:S(2)}) collective-permute-start(bf16[64,1280]{1,0:T(8,128)(2,1)S(1)} %get-tuple-element.59), channel_id=1, source_target_pairs={{0,3},{1,0},{2,1},{3,2},{4,7},{5,4},{6,5},{7,6},{8,11},{9,8},{10,9... | collective-permute-start | bytes 491528 | tf_op jit(solution)/shard_map/ppermute | solution.py:24
  114.7 18.5 %collective-permute-start.25 = (bf16[128,1536]{1,0:T(8,128)(2,1)S(1)}, bf16[128,1536]{1,0:T(8,128)(2,1)S(1)}, u32[]{:S(2)}, u32[]{:S(2)}) collective-permute-start(bf16[128,1536]{1,0:T(8,128)(2,1)S(1)} %shard_map.88), channel_id=1, source_target_pairs={{0,4},{4,8},{8,12},{12,16},{16,20},{20,24},{24,28},{28,32},{32,36}... | collective-permute-start | bytes 1179656 | tf_op jit(solution)/shard_map/ppermute | solution.py:33
  115.3 13.5 %collective-permute-start.17 = (bf16[128,1280]{1,0:T(8,128)(2,1)S(1)}, bf16[128,1280]{1,0:T(8,128)(2,1)S(1)}, u32[]{:S(2)}, u32[]{:S(2)}) collective-permute-start(bf16[128,1280]{1,0:T(8,128)(2,1)S(1)} %shard_map.84), channel_id=1, source_target_pairs={{0,4},{4,8},{8,12},{12,16},{16,20},{20,24},{24,28},{28,32},{32,36}... | collective-permute-start | bytes 983048 | tf_op jit(solution)/shard_map/ppermute | solution.py:33
  117.0 15.3 %collective-permute-start.20 = (bf16[128,1280]{1,0:T(8,128)(2,1)S(1)}, bf16[128,1280]{1,0:T(8,128)(2,1)S(1)}, u32[]{:S(2)}, u32[]{:S(2)}) collective-permute-start(bf16[128,1280]{1,0:T(8,128)(2,1)S(1)} %shard_map.85), channel_id=1, source_target_pairs={{0,4},{4,8},{8,12},{12,16},{16,20},{20,24},{24,28},{28,32},{32,36}... | collective-permute-start | bytes 983048 | tf_op jit(solution)/shard_map/ppermute | solution.py:33
